TPU v7x, 256 devices: a whole 4x4x8 slice. The times are simulated.
256 devices in a mesh: dp: 32 (over z, x_lo, core), expert: 8 (over x_hi, y).
Axes of the slice: x: 4 (x_hi: 2, x_lo: 2; x = x_hi * 2 + x_lo), y: 4, z: 8, core: 2. Of those that a mesh axis runs over, the one named last changes fastest.
Arguments:
- stash: bfloat16 [32768, 6144], P(('dp', 'expert')), may hold values from -24 to 24
- scales: bfloat16 [32768, 48], P(('dp', 'expert')), may hold values from 0.099609375 to 2
- out_grad: bfloat16 [32768, 6144], P(('dp', 'expert')), may hold values from -6 to 6
- route_ids: int32 [32768, 2], P(('dp', 'expert')), may hold values from 0 to 7, as said below
- gates: float32 [32768, 2], P(('dp', 'expert')), may hold values from 0.1 to 1
- w_gate_up: bfloat16 [8, 6144, 512], P('expert'), may hold values from -0.15625 to 0.15625
- w_down: bfloat16 [8, 6144, 256], P('expert', 'dp'), may hold values from -0.078125 to 0.078125
Outputs:
- input_grad: bfloat16 [32768, 6144], P(('dp', 'expert'))
- grad_gate_up: float32 [8, 6144, 512], P('expert', 'dp')
Inputs may be any that keep to these rules, and one draw needn't show every extreme that they name: `route_ids`: each token names two different experts. Within each aligned block of 128 tokens no expert is named more than 56 times. In every run of 8 aligned blocks that starts at a multiple of 8 blocks, some expert is named exactly 56 times in each block of the run.
All inputs are finite; a program needn't handle non-finite values.
Results may differ from a plain program's by a relative error of at most 0.023.
Values may be sent and summed in bfloat16 or wider, within the bound.
A program may use at most 128 MiB of HBM per device.

v0:
```python
import functools

import jax
import jax.numpy as jnp
from jax import lax
from jax.experimental import pallas as pl
from jax.experimental.pallas import tpu as pltpu
from jax.sharding import PartitionSpec as P

MESH = pl.DeviceIdType.MESH


def ring_place():
    index = lax.axis_index("dp")
    return index // 4, lax.rem(index // 2, 2), lax.rem(index, 2)


def greet(partners):
    barrier = pltpu.get_barrier_semaphore()
    for partner in partners:
        pl.semaphore_signal(barrier, inc=1, device_id={"dp": partner}, device_id_type=MESH)
    pl.semaphore_wait(barrier, len(partners))


def gather_kernel(zs, own_ref, out_ref, local_sem, send_sems, recv_sems):
    z, xlo, core = ring_place()

    def at(zz, xx, cc):
        return zz * 4 + xx * 2 + cc

    up, down = lax.rem(z + 1, zs), lax.rem(z + zs - 1, zs)
    to_up, to_down = at(up, xlo, core), at(down, xlo, core)
    to_side, to_twin = at(z, 1 - xlo, core), at(z, xlo, 1 - core)
    greet((to_up, to_down, to_side, to_twin))
    me = at(z, xlo, core)
    keep = pltpu.make_async_copy(own_ref, out_ref.at[me], local_sem)
    keep.start()
    sends = []
    forward = zs // 2
    backward = zs - 1 - forward

    def send(source, piece, number, target):
        copy = pltpu.make_async_remote_copy(
            src_ref=source,
            dst_ref=out_ref.at[piece],
            send_sem=send_sems.at[number],
            recv_sem=recv_sems.at[number],
            device_id={"dp": target},
            device_id_type=MESH,
        )
        copy.start()
        sends.append(copy)

    def arrive(piece, number):
        pltpu.make_async_remote_copy(
            src_ref=own_ref,
            dst_ref=out_ref.at[piece],
            send_sem=send_sems.at[number],
            recv_sem=recv_sems.at[number],
            device_id={"dp": me},
            device_id_type=MESH,
        ).wait_recv()

    ups, downs, twins = 1, 1 + 2 * forward, 1 + 2 * forward + 2 * backward
    send(own_ref, me, 0, to_side)
    send(own_ref, me, ups, to_up)
    send(own_ref, me, downs, to_down)
    send(own_ref, me, twins, to_twin)
    arrive(to_side, 0)
    send(out_ref.at[to_side], to_side, ups + 1, to_up)
    send(out_ref.at[to_side], to_side, downs + 1, to_down)
    send(out_ref.at[to_side], to_side, twins + 1, to_twin)
    for hop in range(1, forward + 1):
        for pair in range(2):
            xx = xlo if pair == 0 else 1 - xlo
            piece = at(lax.rem(z + zs - hop, zs), xx, core)
            arrive(piece, ups + 2 * (hop - 1) + pair)
            if hop < forward:
                send(out_ref.at[piece], piece, ups + 2 * hop + pair, to_up)
            send(out_ref.at[piece], piece, twins + 2 * hop + pair, to_twin)
            if hop <= backward:
                piece = at(lax.rem(z + hop, zs), xx, core)
                arrive(piece, downs + 2 * (hop - 1) + pair)
                if hop < backward:
                    send(out_ref.at[piece], piece, downs + 2 * hop + pair, to_down)
                send(out_ref.at[piece], piece, twins + 2 * (forward + hop) + pair, to_twin)
    for pair in range(2):
        xx = xlo if pair == 0 else 1 - xlo
        arrive(at(z, xx, 1 - core), twins + pair)
        for hop in range(1, forward + 1):
            arrive(at(lax.rem(z + zs - hop, zs), xx, 1 - core), twins + 2 * hop + pair)
        for hop in range(1, backward + 1):
            arrive(at(lax.rem(z + hop, zs), xx, 1 - core), twins + 2 * (forward + hop) + pair)
    for copy in sends:
        copy.wait_send()
    keep.wait()


def gather_rows(own, dp_count, collective_id):
    zs = dp_count // 4
    copies = 1 + 2 * (zs - 1) + 2 * zs
    return pl.pallas_call(
        functools.partial(gather_kernel, zs),
        out_shape=jax.ShapeDtypeStruct((dp_count,) + own.shape, own.dtype),
        in_specs=[pl.BlockSpec(memory_space=pltpu.VMEM)],
        out_specs=pl.BlockSpec(memory_space=pl.ANY),
        scratch_shapes=[
            pltpu.SemaphoreType.DMA,
            pltpu.SemaphoreType.DMA((copies,)),
            pltpu.SemaphoreType.DMA((copies,)),
        ],
        compiler_params=pltpu.CompilerParams(collective_id=collective_id, has_side_effects=True),
        cost_estimate=pl.CostEstimate(flops=20_000_000_000, bytes_accessed=3_000_000, transcendentals=0),
        name="gather_rows",
    )(own)


def reduce_kernel(zs, subs, part_ref, out_ref, core_ref, ring_ref, stage_ref, side_ref,
                  core_send, core_recv, ring_send, ring_recv, side_send, side_recv):
    z, xlo, core = ring_place()
    rows = part_ref.shape[1]
    step_rows = rows // subs

    def at(zz, xx, cc):
        return zz * 4 + xx * 2 + cc

    up, down = lax.rem(z + 1, zs), lax.rem(z + zs - 1, zs)
    to_up, to_down = at(up, xlo, core), at(down, xlo, core)
    to_side, to_twin = at(z, 1 - xlo, core), at(z, xlo, 1 - core)
    greet((to_up, to_down, to_side, to_twin))

    def owner(way, step):
        return lax.rem(z + 2 * zs - 1 - step, zs) if way == 0 else lax.rem(z + 1 + step, zs)

    def core_copy(way, step):
        piece = owner(way, step)
        return pltpu.make_async_remote_copy(
            src_ref=part_ref.at[at(piece, way, 1 - core)],
            dst_ref=core_ref.at[way, step],
            send_sem=core_send.at[way, step],
            recv_sem=core_recv.at[way, step],
            device_id={"dp": to_twin},
            device_id_type=MESH,
        )

    def ring_copy(way, step, sub):
        return pltpu.make_async_remote_copy(
            src_ref=stage_ref.at[way, step, sub],
            dst_ref=ring_ref.at[way, step, sub],
            send_sem=ring_send.at[way, step, sub],
            recv_sem=ring_recv.at[way, step, sub],
            device_id={"dp": to_up if way == 0 else to_down},
            device_id_type=MESH,
        )

    def side_copy(sub):
        return pltpu.make_async_remote_copy(
            src_ref=stage_ref.at[1 - xlo, zs - 1, sub],
            dst_ref=side_ref.at[sub],
            send_sem=side_send.at[sub],
            recv_sem=side_recv.at[sub],
            device_id={"dp": to_side},
            device_id_type=MESH,
        )

    for step in range(zs):
        for way in range(2):
            core_copy(way, step).start()
    for step in range(zs):
        for sub in range(subs):
            for way in range(2):
                if sub == 0:
                    core_copy(way, step).wait_recv()
                piece = at(owner(way, step), way, core)
                span = pl.ds(sub * step_rows, step_rows)
                value = part_ref[piece, span, :].astype(jnp.float32) + core_ref[way, step, span, :].astype(jnp.float32)
                if step > 0:
                    ring_copy(way, step - 1, sub).wait_recv()
                    value = value + ring_ref[way, step - 1, sub].astype(jnp.float32)
                stage_ref[way, step, sub] = value.astype(stage_ref.dtype)
                if step < zs - 1:
                    ring_copy(way, step, sub).start()
        if step == zs - 1:
            for sub in range(subs):
                side_copy(sub).start()
    share = 1.0 / (4 * zs)
    for sub in range(subs):
        side_copy(sub).wait_recv()
        span = pl.ds(sub * step_rows, step_rows)
        total = stage_ref[xlo, zs - 1, sub].astype(jnp.float32) + side_ref[sub].astype(jnp.float32)
        out_ref[span, :] = total * share
    for step in range(zs):
        for way in range(2):
            core_copy(way, step).wait_send()
            for sub in range(subs):
                if step < zs - 1:
                    ring_copy(way, step, sub).wait_send()
    for sub in range(subs):
        side_copy(sub).wait_send()


def reduce_rows(part, dp_count, collective_id, subs=2):
    zs = dp_count // 4
    width = part.shape[1]
    rows = part.shape[0] // dp_count
    kind = part.dtype
    return pl.pallas_call(
        functools.partial(reduce_kernel, zs, subs),
        out_shape=jax.ShapeDtypeStruct((rows, width), jnp.float32),
        in_specs=[pl.BlockSpec(memory_space=pltpu.VMEM)],
        out_specs=pl.BlockSpec(memory_space=pltpu.VMEM),
        scratch_shapes=[
            pltpu.VMEM((2, zs, rows, width), kind),
            pltpu.VMEM((2, zs - 1, subs, rows // subs, width), kind),
            pltpu.VMEM((2, zs, subs, rows // subs, width), kind),
            pltpu.VMEM((subs, rows // subs, width), kind),
            pltpu.SemaphoreType.DMA((2, zs)),
            pltpu.SemaphoreType.DMA((2, zs)),
            pltpu.SemaphoreType.DMA((2, zs - 1, subs)),
            pltpu.SemaphoreType.DMA((2, zs - 1, subs)),
            pltpu.SemaphoreType.DMA((subs,)),
            pltpu.SemaphoreType.DMA((subs,)),
        ],
        compiler_params=pltpu.CompilerParams(
            collective_id=collective_id, has_side_effects=True, vmem_limit_bytes=32 * 1024 * 1024
        ),
        cost_estimate=pl.CostEstimate(flops=40_000_000_000, bytes_accessed=7_000_000, transcendentals=0),
        name="reduce_rows",
    )(part.reshape(dp_count, rows, width))


def dispatch_masks(route_ids, experts, capacity):
    tokens = route_ids.shape[0]
    flat_ids = route_ids.reshape(-1)
    slot_total = flat_ids.shape[0]
    onehot = flat_ids[:, None] == jnp.arange(experts, dtype=jnp.int32)[None, :]
    order = jnp.arange(slot_total, dtype=jnp.int32)
    before = (order[:, None] > order[None, :]).astype(jnp.bfloat16)
    earlier = jnp.dot(before, onehot.astype(jnp.bfloat16), preferred_element_type=jnp.float32)
    ranking = jnp.sum(jnp.where(onehot, earlier, 0.0), axis=1).astype(jnp.int32)
    destination = (flat_ids * capacity + ranking).reshape(tokens, 2)
    rows = jnp.arange(experts * capacity, dtype=jnp.int32)
    first = rows[:, None] == destination[:, 0][None, :]
    second = rows[:, None] == destination[:, 1][None, :]
    return first, second


def dequantize(stash_rows, scale_rows):
    row_total = stash_rows.shape[0]
    blocks = scale_rows.shape[1]
    scaled = (
        stash_rows.reshape(row_total, blocks, -1).astype(jnp.float32)
        * scale_rows.astype(jnp.float32)[:, :, None]
    )
    return scaled.reshape(row_total, -1).astype(jnp.bfloat16)


def gated_backward(gate_up, back_hidden):
    hidden = back_hidden.shape[1]
    gate_value = gate_up[:, :hidden]
    up_value = gate_up[:, hidden:]
    sigmoid_gate = jax.nn.sigmoid(gate_value)
    grad_gate = back_hidden * up_value * sigmoid_gate * (1.0 + gate_value * (1.0 - sigmoid_gate))
    grad_up = back_hidden * gate_value * sigmoid_gate
    return jnp.concatenate([grad_gate, grad_up], axis=1).astype(jnp.bfloat16)


def exchange(rows, experts, capacity):
    width = rows.shape[1]
    moved = lax.all_to_all(
        rows.reshape(experts, capacity, width), "expert", split_axis=0, concat_axis=0, tiled=True
    )
    return moved.reshape(experts * capacity, width)


def on_device(stash, scales, out_grad, route_ids, gates, w_gate_up, w_down):
    tokens, feature_width = stash.shape
    hidden = w_down.shape[2]
    experts = lax.axis_size("expert")
    dp_count = lax.axis_size("dp")
    capacity = min(tokens, 7 * tokens // (2 * experts))
    first, second = dispatch_masks(route_ids, experts, capacity)
    picks = (first | second).astype(jnp.bfloat16)
    row_gate = jnp.sum(
        jnp.where(first, gates[:, 0][None, :], 0.0) + jnp.where(second, gates[:, 1][None, :], 0.0), axis=1
    )
    sent_x = jnp.dot(picks, dequantize(stash, scales), preferred_element_type=jnp.float32).astype(jnp.bfloat16)
    sent_grad = (
        jnp.dot(picks, out_grad, preferred_element_type=jnp.float32) * row_gate[:, None]
    ).astype(jnp.bfloat16)
    weight_in = w_gate_up[0]
    features = exchange(sent_x, experts, capacity)
    gate_up = jnp.dot(features, weight_in, preferred_element_type=jnp.float32)
    upstream = exchange(sent_grad, experts, capacity)
    weight_out = gather_rows(w_down[0], dp_count, 1).reshape(feature_width, hidden)
    back_hidden = jnp.dot(upstream, weight_out, preferred_element_type=jnp.float32)
    hidden_grad = gated_backward(gate_up, back_hidden)
    slot_grads = lax.dot_general(
        hidden_grad, weight_in, (((1,), (1,)), ((), ())), preferred_element_type=jnp.float32
    ).astype(jnp.bfloat16)
    returned = exchange(slot_grads, experts, capacity)
    input_grad = lax.dot_general(
        picks, returned, (((0,), (0,)), ((), ())), preferred_element_type=jnp.float32
    ).astype(jnp.bfloat16)
    local_rows = feature_width // dp_count
    partial_grad = lax.dot_general(
        features, hidden_grad, (((0,), (0,)), ((), ())), preferred_element_type=jnp.float32
    ).astype(jnp.bfloat16)
    grad_gate_up = reduce_rows(partial_grad, dp_count, 2).reshape(1, local_rows, 2 * hidden)
    return (input_grad, grad_gate_up)


def solution(mesh):
    placed = (
        P(("dp", "expert"), None),
        P(("dp", "expert"), None),
        P(("dp", "expert"), None),
        P(("dp", "expert"), None),
        P(("dp", "expert"), None),
        P("expert", None, None),
        P("expert", "dp", None),
    )
    return jax.shard_map(
        on_device,
        mesh=mesh,
        in_specs=placed,
        out_specs=(P(("dp", "expert"), None), P("expert", "dp", None)),
        check_vma=False,
    )
```

profile of v0, /device:TPU:4, one launch (start us, length us, event | category | flops | bytes accessed | tf_op | source)
XLA Modules:
  0.0 271.9 jit_solution(7698581750840328951)
XLA Ops:
  0.6 0.0 copy-start
  0.6 0.9 copy.22
  1.5 0.1 eq.46
  1.7 0.2 fusion.5
  1.9 0.1 convert_element_type.37
  2.0 0.1 copy.23
  2.1 0.7 multiply_add_fusion
  2.8 0.8 copy.24
  3.6 0.9 mul.48
  4.5 5.5 %convolution_convert_fusion.2 = bf16[448,6144]{1,0:T(8,128)(2,1)} fusion(f32[16,8,48,128]{3,2,1,0:T(8,128)S(1)} %bitcast.39, bf16[128,6144]{1,0:T(8,128)(2,1)} %param.7, s32[128]{0:T(128)S(1)} %get-tuple-element.5, s32[128]{0:T(128)S(1)} %get-tuple-element.4), kind=kOutput, calls=%fused_computation.3 | convolution fusion | flops 709926912 | bytes 10224640 | tf_op jit(solution)/shard_map/dot_general | solution.py:287
  10.0 7.6 %all-to-all-start.1 = ((bf16[8,56,6144]{2,1,0:T(8,128)(2,1)}), bf16[8,56,6144]{2,1,0:T(8,128)(2,1)}, u32[]{:S(2)}, u32[]{:S(2)}) async-start(bf16[8,56,6144]{2,1,0:T(8,128)(2,1)} %bitcast.37), calls=%async_computation.1 | async-start | bytes 11010048 | tf_op jit(solution)/shard_map/all_to_all | solution.py:270
  17.6 0.1 add_reduce_fusion
  17.7 4.0 %multiply_convert_fusion = bf16[448,6144]{1,0:T(8,128)(2,1)} fusion(bf16[128,6144]{1,0:T(8,128)(2,1)S(1)} %copy-done, f32[448]{0:T(512)S(1)} %add_reduce_fusion, s32[128]{0:T(128)S(1)} %get-tuple-element.5, s32[128]{0:T(128)S(1)} %get-tuple-element.4), kind=kOutput, calls=%fused_computation | convolution fusion | flops 710320128 | bytes 7080704 | tf_op jit(solution)/shard_map/dot_general | solution.py:289
  21.8 57.9 %all-to-all-done.1 = bf16[8,56,6144]{2,1,0:T(8,128)(2,1)} async-done(((bf16[8,56,6144]{2,1,0:T(8,128)(2,1)}), bf16[8,56,6144]{2,1,0:T(8,128)(2,1)}, u32[]{:S(2)}, u32[]{:S(2)}) %all-to-all-start.1) | async-done | bytes 5505056 | tf_op jit(solution)/shard_map/all_to_all | solution.py:270
  79.6 5.7 %all-to-all-start = ((bf16[8,56,6144]{2,1,0:T(8,128)(2,1)}), bf16[8,56,6144]{2,1,0:T(8,128)(2,1)}, u32[]{:S(2)}, u32[]{:S(2)}) async-start(bf16[8,56,6144]{2,1,0:T(8,128)(2,1)} %bitcast.38), calls=%async_computation | async-start | bytes 11010048 | tf_op jit(solution)/shard_map/all_to_all | solution.py:270
  85.3 87.9 %gather_rows.1 = bf16[32,192,256]{2,1,0:T(8,128)(2,1)} custom-call(bf16[192,256]{1,0:T(8,128)(2,1)} %bitcast.41), custom_call_target="tpu_custom_call" | custom-call | flops 20000000000 | bytes 3000000 | tf_op jit(solution)/shard_map/gather_rows/pallas_call | solution.py:102
  173.2 6.8 %fusion.1 = f32[448,512]{1,0:T(8,128)S(1)} fusion(bf16[448,6144]{1,0:T(8,128)(2,1)} %bitcast.9, bf16[1,6144,512]{2,1,0:T(8,128)(2,1)} %param.12), kind=kOutput, calls=%fused_computation.6 | convolution fusion | flops 2818572288 | bytes 12713984 | tf_op jit(solution)/shard_map/dot_general | solution.py:293
  180.1 5.2 %fusion.8 = (bf16[448,256]{1,0:T(8,128)(2,1)S(1)}, bf16[448,256]{1,0:T(8,128)(2,1)S(1)}) fusion(f32[448,512]{1,0:T(8,128)S(1)} %fusion.1, bf16[448,6144]{1,0:T(8,128)(2,1)} %bitcast.5, bf16[6144,256]{1,0:T(8,128)(2,1)} %bitcast.42), kind=kOutput, calls=%fused_computation.15 | convolution fusion | flops 1410777088 | bytes 10027008 | tf_op jit(solution)/shard_map/dot_general | solution.py:296
  185.2 8.4 %convolution_convert_fusion.1 = bf16[448,6144]{1,0:T(8,128)(2,1)} fusion(bf16[1,6144,512]{2,1,0:T(8,128)(2,1)} %param.12, bf16[448,256]{1,0:T(8,128)(2,1)S(1)} %get-tuple-element.3, bf16[448,256]{1,0:T(8,128)(2,1)S(1)} %get-tuple-element.2), kind=kOutput, calls=%fused_computation.2 | convolution fusion | flops 2822242304 | bytes 12255232 | tf_op jit(solution)/shard_map/dot_general | solution.py:298
  193.6 6.4 %all-to-all-start.2 = ((bf16[8,56,6144]{2,1,0:T(8,128)(2,1)}), bf16[8,56,6144]{2,1,0:T(8,128)(2,1)}, u32[]{:S(2)}, u32[]{:S(2)}) async-start(bf16[8,56,6144]{2,1,0:T(8,128)(2,1)} %bitcast.40), calls=%async_computation.2 | async-start | bytes 11010048 | tf_op jit(solution)/shard_map/all_to_all | solution.py:270
  199.9 6.5 %convolution_convert_fusion = bf16[6144,512]{1,0:T(8,128)(2,1)S(1)} fusion(bf16[448,6144]{1,0:T(8,128)(2,1)} %bitcast.9, bf16[448,256]{1,0:T(8,128)(2,1)S(1)} %get-tuple-element.3, bf16[448,256]{1,0:T(8,128)(2,1)S(1)} %get-tuple-element.2), kind=kOutput, calls=%fused_computation.1 | convolution fusion | flops 2822635520 | bytes 12255232 | tf_op jit(solution)/shard_map/dot_general | solution.py:306
  206.5 59.9 %reduce_rows.1 = f32[192,512]{1,0:T(8,128)S(1)} custom-call(bf16[32,192,512]{2,1,0:T(8,128)(2,1)S(1)} %bitcast.36), custom_call_target="tpu_custom_call" | custom-call | flops 40000000000 | bytes 7000000 | tf_op jit(solution)/shard_map/reduce_rows/pallas_call | solution.py:207
  266.4 4.7 %convolution_convert_fusion.3 = bf16[128,6144]{1,0:T(8,128)(2,1)} fusion(bf16[448,6144]{1,0:T(8,128)(2,1)} %bitcast.12, s32[128]{0:T(128)S(1)} %get-tuple-element.5, s32[128]{0:T(128)S(1)} %get-tuple-element.4), kind=kOutput, calls=%fused_computation.4 | convolution fusion | flops 705601536 | bytes 7078912 | tf_op jit(solution)/shard_map/dot_general | solution.py:302
  271.2 0.7 copy.29
  (8 shorter events, 0.0 us)
Async XLA Ops:
  0.6 17.1 %copy-start = (bf16[128,6144]{1,0:T(8,128)(2,1)S(1)}, bf16[128,6144]{1,0:T(8,128)(2,1)}, u32[]{:S(2)}) copy-start(bf16[128,6144]{1,0:T(8,128)(2,1)} %param.9) | copy-start | bytes 4718596
  10.0 7.6 %copy-start.1 = (f32[128,2]{0,1:T(2,128)S(1)}, f32[128,2]{0,1:T(2,128)}, u32[]{:S(2)}) copy-start(f32[128,2]{0,1:T(2,128)} %param.11) | copy-start | bytes 3076
  10.0 69.7 %all-to-all-start.1 = ((bf16[8,56,6144]{2,1,0:T(8,128)(2,1)}), bf16[8,56,6144]{2,1,0:T(8,128)(2,1)}, u32[]{:S(2)}, u32[]{:S(2)}) async-start(bf16[8,56,6144]{2,1,0:T(8,128)(2,1)} %bitcast.37), calls=%async_computation.1 | async-start | bytes 11010048 | tf_op jit(solution)/shard_map/all_to_all | solution.py:270
  79.6 100.4 %all-to-all-start = ((bf16[8,56,6144]{2,1,0:T(8,128)(2,1)}), bf16[8,56,6144]{2,1,0:T(8,128)(2,1)}, u32[]{:S(2)}, u32[]{:S(2)}) async-start(bf16[8,56,6144]{2,1,0:T(8,128)(2,1)} %bitcast.38), calls=%async_computation | async-start | bytes 11010048 | tf_op jit(solution)/shard_map/all_to_all | solution.py:270
  193.6 72.8 %all-to-all-start.2 = ((bf16[8,56,6144]{2,1,0:T(8,128)(2,1)}), bf16[8,56,6144]{2,1,0:T(8,128)(2,1)}, u32[]{:S(2)}, u32[]{:S(2)}) async-start(bf16[8,56,6144]{2,1,0:T(8,128)(2,1)} %bitcast.40), calls=%async_computation.2 | async-start | bytes 11010048 | tf_op jit(solution)/shard_map/all_to_all | solution.py:270
where the time goes:
time: 272 us
  Pallas kernels  148 us (54%)
  waiting for transfers between devices  57.9 us (21%)
  matrix products  41.3 us (15%)
  starting transfers between devices  19.6 us (7%)
  local copies, waits for them, and re-layouts  3.68 us (1%)
    pallas_call x1, Pallas kernels, gather_rows(): pl.pallas_call(functools.partial(gather_kernel, zs), out_shape=jax.ShapeD...  87.9 us
    pallas_call x1, Pallas kernels, reduce_rows(): pl.pallas_call(functools.partial(reduce_kernel, zs, subs), out_shape=jax....  59.9 us
    all_to_all x3, waiting for transfers between devices, exchange(): lax.all_to_all(rows.reshape(experts, capacity, width), 'expert', split_ax...  57.9 us
    all_to_all x3, starting transfers between devices, exchange(): lax.all_to_all(rows.reshape(experts, capacity, width), 'expert', split_ax...  19.6 us
    dot_general x1, matrix products, on_device(): lax.dot_general(hidden_grad, weight_in, (((1,), (1,)), ((), ())), preferr...  8.36 us
    dot_general x1, matrix products, on_device(): gate_up = jnp.dot(features, weight_in, preferred_element_type=jnp.float32)  6.81 us
    dot_general x1, matrix products, on_device(): lax.dot_general(features, hidden_grad, (((0,), (0,)), ((), ())), preferre...  6.52 us
    dot_general x1, matrix products, on_device(): jnp.dot(picks, dequantize(stash, scales), preferred_element_type=jnp.floa...  5.48 us
  transfers between devices with their start and end apart: 3, of which 1 were waited for; matrix products, arithmetic and copies ran while one was open for 6% of the time, Pallas kernels for 54%

commit v1 on v0

v1 whole, which is shorter than its diff:
```python
import functools

import jax
import jax.numpy as jnp
from jax import lax
from jax.experimental import pallas as pl
from jax.experimental.pallas import tpu as pltpu
from jax.sharding import Mesh
from jax.sharding import PartitionSpec as P

MESH = pl.DeviceIdType.MESH
COLUMN_AXES = ("z", "xlo", "core")
ROW_AXES = ("xhi", "y")


def ring_place():
    return lax.axis_index("z"), lax.axis_index("xlo"), lax.axis_index("core")


def place(z, xlo, core):
    return {"z": z, "xlo": xlo, "core": core}


def greet(partners):
    barrier = pltpu.get_barrier_semaphore()
    for partner in partners:
        pl.semaphore_signal(barrier, inc=1, device_id=partner, device_id_type=MESH)
    pl.semaphore_wait(barrier, len(partners))


def reduce_kernel(zs, subs, part_ref, out_ref, core_ref, ring_ref, stage_ref, side_ref,
                  core_send, core_recv, ring_send, ring_recv, side_send, side_recv):
    z, xlo, core = ring_place()
    rows = part_ref.shape[1]
    step_rows = rows // subs

    def at(zz, xx, cc):
        return zz * 4 + xx * 2 + cc

    up, down = lax.rem(z + 1, zs), lax.rem(z + zs - 1, zs)
    to_up, to_down = place(up, xlo, core), place(down, xlo, core)
    to_side, to_twin = place(z, 1 - xlo, core), place(z, xlo, 1 - core)
    greet((to_up, to_down, to_side, to_twin))

    def owner(way, step):
        return lax.rem(z + 2 * zs - 1 - step, zs) if way == 0 else lax.rem(z + 1 + step, zs)

    def core_copy(way, step):
        piece = owner(way, step)
        return pltpu.make_async_remote_copy(
            src_ref=part_ref.at[at(piece, way, 1 - core)],
            dst_ref=core_ref.at[way, step],
            send_sem=core_send.at[way, step],
            recv_sem=core_recv.at[way, step],
            device_id=to_twin,
            device_id_type=MESH,
        )

    def ring_copy(way, step, sub):
        return pltpu.make_async_remote_copy(
            src_ref=stage_ref.at[way, step, sub],
            dst_ref=ring_ref.at[way, step, sub],
            send_sem=ring_send.at[way, step, sub],
            recv_sem=ring_recv.at[way, step, sub],
            device_id=to_up if way == 0 else to_down,
            device_id_type=MESH,
        )

    def side_copy(sub):
        return pltpu.make_async_remote_copy(
            src_ref=stage_ref.at[1 - xlo, zs - 1, sub],
            dst_ref=side_ref.at[sub],
            send_sem=side_send.at[sub],
            recv_sem=side_recv.at[sub],
            device_id=to_side,
            device_id_type=MESH,
        )

    for step in range(zs):
        for way in range(2):
            core_copy(way, step).start()
    for step in range(zs):
        for sub in range(subs):
            for way in range(2):
                if sub == 0:
                    core_copy(way, step).wait_recv()
                piece = at(owner(way, step), way, core)
                span = pl.ds(sub * step_rows, step_rows)
                value = part_ref[piece, span, :].astype(jnp.float32) + core_ref[way, step, span, :].astype(jnp.float32)
                if step > 0:
                    ring_copy(way, step - 1, sub).wait_recv()
                    value = value + ring_ref[way, step - 1, sub].astype(jnp.float32)
                stage_ref[way, step, sub] = value.astype(stage_ref.dtype)
                if step < zs - 1:
                    ring_copy(way, step, sub).start()
        if step == zs - 1:
            for sub in range(subs):
                side_copy(sub).start()
    share = 1.0 / (4 * zs)
    for sub in range(subs):
        side_copy(sub).wait_recv()
        span = pl.ds(sub * step_rows, step_rows)
        total = stage_ref[xlo, zs - 1, sub].astype(jnp.float32) + side_ref[sub].astype(jnp.float32)
        out_ref[span, :] = total * share
    for step in range(zs):
        for way in range(2):
            core_copy(way, step).wait_send()
            for sub in range(subs):
                if step < zs - 1:
                    ring_copy(way, step, sub).wait_send()
    for sub in range(subs):
        side_copy(sub).wait_send()


def reduce_rows(part, dp_count, collective_id, subs=2):
    zs = dp_count // 4
    width = part.shape[1]
    rows = part.shape[0] // dp_count
    kind = part.dtype
    return pl.pallas_call(
        functools.partial(reduce_kernel, zs, subs),
        out_shape=jax.ShapeDtypeStruct((rows, width), jnp.float32),
        in_specs=[pl.BlockSpec(memory_space=pltpu.VMEM)],
        out_specs=pl.BlockSpec(memory_space=pltpu.VMEM),
        scratch_shapes=[
            pltpu.VMEM((2, zs, rows, width), kind),
            pltpu.VMEM((2, zs - 1, subs, rows // subs, width), kind),
            pltpu.VMEM((2, zs, subs, rows // subs, width), kind),
            pltpu.VMEM((subs, rows // subs, width), kind),
            pltpu.SemaphoreType.DMA((2, zs)),
            pltpu.SemaphoreType.DMA((2, zs)),
            pltpu.SemaphoreType.DMA((2, zs - 1, subs)),
            pltpu.SemaphoreType.DMA((2, zs - 1, subs)),
            pltpu.SemaphoreType.DMA((subs,)),
            pltpu.SemaphoreType.DMA((subs,)),
        ],
        compiler_params=pltpu.CompilerParams(
            collective_id=collective_id, has_side_effects=True, vmem_limit_bytes=32 * 1024 * 1024
        ),
        cost_estimate=pl.CostEstimate(flops=40_000_000_000, bytes_accessed=7_000_000, transcendentals=0),
        name="reduce_rows",
    )(part.reshape(dp_count, rows, width))


def dispatch_masks(route_ids, experts, capacity):
    tokens = route_ids.shape[0]
    flat_ids = route_ids.reshape(-1)
    slot_total = flat_ids.shape[0]
    onehot = flat_ids[:, None] == jnp.arange(experts, dtype=jnp.int32)[None, :]
    order = jnp.arange(slot_total, dtype=jnp.int32)
    before = (order[:, None] > order[None, :]).astype(jnp.bfloat16)
    earlier = jnp.dot(before, onehot.astype(jnp.bfloat16), preferred_element_type=jnp.float32)
    ranking = jnp.sum(jnp.where(onehot, earlier, 0.0), axis=1).astype(jnp.int32)
    destination = (flat_ids * capacity + ranking).reshape(tokens, 2)
    rows = jnp.arange(experts * capacity, dtype=jnp.int32)
    first = rows[:, None] == destination[:, 0][None, :]
    second = rows[:, None] == destination[:, 1][None, :]
    return first, second


def dequantize(stash_rows, scale_rows):
    row_total = stash_rows.shape[0]
    blocks = scale_rows.shape[1]
    scaled = (
        stash_rows.reshape(row_total, blocks, -1).astype(jnp.float32)
        * scale_rows.astype(jnp.float32)[:, :, None]
    )
    return scaled.reshape(row_total, -1).astype(jnp.bfloat16)


def gated_backward(gate_up, back_hidden):
    hidden = back_hidden.shape[1]
    gate_value = gate_up[:, :hidden]
    up_value = gate_up[:, hidden:]
    sigmoid_gate = jax.nn.sigmoid(gate_value)
    grad_gate = back_hidden * up_value * sigmoid_gate * (1.0 + gate_value * (1.0 - sigmoid_gate))
    grad_up = back_hidden * gate_value * sigmoid_gate
    return jnp.concatenate([grad_gate, grad_up], axis=1).astype(jnp.bfloat16)


def exchange(rows, experts, capacity):
    width = rows.shape[1]
    moved = lax.all_to_all(
        rows.reshape(experts, capacity, width), ROW_AXES, split_axis=0, concat_axis=0, tiled=True
    )
    return moved.reshape(experts * capacity, width)


def plane_weights(w_down):
    planes = lax.axis_size("xlo")
    experts = lax.axis_size(ROW_AXES)
    copies = jnp.broadcast_to(w_down[None], (planes * experts,) + w_down.shape)
    mine = lax.all_to_all(copies, ("xlo",) + ROW_AXES, split_axis=0, concat_axis=0, tiled=True)
    return mine.reshape((planes, experts) + w_down.shape)


def relay_kernel(zs, grad_ref, ids_ref, gate_ref, weight_ref, out_ref,
                 slice_ref, wide_ref, pick_ref, stage_ref, back_ref,
                 own_sem, slice_send, slice_recv, weight_sem, weight_send, weight_recv, back_send, back_recv):
    z, xlo, core = ring_place()
    tokens = out_ref.shape[1]
    depth = slice_ref.shape[2]
    experts = weight_ref.shape[1]
    rows = weight_ref.shape[2]
    half = zs // 2
    offsets = []
    for d in range(1, half):
        offsets += [-d, d]
    offsets += [half, 0]
    twin = place(z, xlo, 1 - core)

    def peer(offset):
        return lax.rem(z + offset + zs, zs)

    def mirror(slot):
        return slot if slot >= zs - 2 else slot ^ 1

    greet([place(peer(offset), xlo, core) for offset in offsets[:-1]] + [twin])

    def columns(offset):
        return pl.ds(pl.multiple_of(peer(offset) * depth, depth), depth)

    def slice_copy(slot):
        return pltpu.make_async_remote_copy(
            src_ref=grad_ref.at[:, columns(offsets[slot])],
            dst_ref=slice_ref.at[mirror(slot)],
            send_sem=slice_send.at[slot],
            recv_sem=slice_recv.at[mirror(slot)],
            device_id=place(peer(offsets[slot]), xlo, core),
            device_id_type=MESH,
        )

    def back_copy(slot):
        return pltpu.make_async_remote_copy(
            src_ref=stage_ref.at[slot],
            dst_ref=back_ref.at[mirror(slot)],
            send_sem=back_send.at[slot],
            recv_sem=back_recv.at[mirror(slot)],
            device_id=place(peer(offsets[slot]), xlo, core),
            device_id_type=MESH,
        )

    def slice_arrival(slot):
        return pltpu.make_async_remote_copy(
            src_ref=slice_ref.at[slot],
            dst_ref=slice_ref.at[slot],
            send_sem=slice_send.at[slot],
            recv_sem=slice_recv.at[slot],
            device_id=twin,
            device_id_type=MESH,
        )

    def back_arrival(slot):
        return pltpu.make_async_remote_copy(
            src_ref=back_ref.at[slot],
            dst_ref=back_ref.at[slot],
            send_sem=back_send.at[slot],
            recv_sem=back_recv.at[slot],
            device_id=twin,
            device_id_type=MESH,
        )

    def weight_rows(plane, side):
        return wide_ref.at[:, pl.ds(pl.multiple_of((2 * plane + side) * rows, rows), rows), :]

    def weight_copy(plane):
        return pltpu.make_async_remote_copy(
            src_ref=weight_ref.at[plane],
            dst_ref=weight_rows(plane, core),
            send_sem=weight_send.at[plane],
            recv_sem=weight_recv.at[plane],
            device_id=twin,
            device_id_type=MESH,
        )

    def weight_arrival(plane):
        return pltpu.make_async_remote_copy(
            src_ref=weight_ref.at[plane],
            dst_ref=weight_rows(plane, 1 - core),
            send_sem=weight_send.at[plane],
            recv_sem=weight_recv.at[plane],
            device_id=twin,
            device_id_type=MESH,
        )

    keeps = [pltpu.make_async_copy(grad_ref.at[:, columns(0)], slice_ref.at[zs - 1], own_sem)]
    for plane in range(2):
        keeps.append(pltpu.make_async_copy(weight_ref.at[plane], weight_rows(plane, core), weight_sem.at[plane]))
    for slot in range(zs - 1):
        slice_copy(slot).start()
    for plane in range(2):
        weight_copy(plane).start()
    for keep in keeps:
        keep.start()
    for keep in keeps:
        keep.wait()
    for plane in range(2):
        weight_arrival(plane).wait_recv()
    for pair in range(half):
        for side in range(2):
            slot = 2 * pair + side
            if slot < zs - 1:
                slice_arrival(slot).wait_recv()
        pick_ref[...] = jnp.zeros_like(pick_ref)

        def per_expert(e, carry):
            wide = wide_ref[e]
            for side in range(2):
                slot = 2 * pair + side
                dense = jnp.dot(slice_ref[slot], wide, preferred_element_type=jnp.float32)
                first_row = pl.multiple_of(peer(offsets[slot]) * tokens, tokens)
                for k in range(2):
                    chosen = ids_ref[pl.ds(first_row, tokens), k : k + 1] == e
                    pick_ref[side, k] = jnp.where(chosen, dense, pick_ref[side, k])
            return carry

        lax.fori_loop(0, experts, per_expert, 0)
        for side in range(2):
            slot = 2 * pair + side
            stage_ref[slot] = pick_ref[side].astype(stage_ref.dtype)
            if slot < zs - 1:
                back_copy(slot).start()
    total = stage_ref[zs - 1].astype(jnp.float32)
    for slot in range(zs - 1):
        back_arrival(slot).wait_recv()
        total = total + back_ref[slot].astype(jnp.float32)
    for k in range(2):
        out_ref[k] = (total[k] * gate_ref[:, k : k + 1]).astype(out_ref.dtype)
    for slot in range(zs - 1):
        slice_copy(slot).wait_send()
        back_copy(slot).wait_send()
    for plane in range(2):
        weight_copy(plane).wait_send()


def hidden_gradient(out_grad, all_ids, gates, weights, zs):
    tokens, feature_width = out_grad.shape
    planes, experts, rows, hidden = weights.shape
    depth = feature_width // zs
    kind = out_grad.dtype
    vmem = pl.BlockSpec(memory_space=pltpu.VMEM)
    return pl.pallas_call(
        functools.partial(relay_kernel, zs),
        out_shape=jax.ShapeDtypeStruct((2, tokens, hidden), kind),
        in_specs=[pl.BlockSpec(memory_space=pl.ANY), vmem, vmem, pl.BlockSpec(memory_space=pl.ANY)],
        out_specs=vmem,
        scratch_shapes=[
            pltpu.VMEM((zs, tokens, depth), kind),
            pltpu.VMEM((experts, 2 * planes * rows, hidden), kind),
            pltpu.VMEM((2, 2, tokens, hidden), jnp.float32),
            pltpu.VMEM((zs, 2, tokens, hidden), kind),
            pltpu.VMEM((zs - 1, 2, tokens, hidden), kind),
            pltpu.SemaphoreType.DMA,
            pltpu.SemaphoreType.DMA((zs - 1,)),
            pltpu.SemaphoreType.DMA((zs - 1,)),
            pltpu.SemaphoreType.DMA((2,)),
            pltpu.SemaphoreType.DMA((2,)),
            pltpu.SemaphoreType.DMA((2,)),
            pltpu.SemaphoreType.DMA((zs - 1,)),
            pltpu.SemaphoreType.DMA((zs - 1,)),
        ],
        compiler_params=pltpu.CompilerParams(
            collective_id=1, has_side_effects=True, vmem_limit_bytes=24 * 1024 * 1024
        ),
        cost_estimate=pl.CostEstimate(flops=40_000_000_000, bytes_accessed=7_000_000, transcendentals=0),
        name="relay_hidden",
    )(out_grad, all_ids, gates, weights)


def on_device(stash, scales, out_grad, route_ids, gates, w_gate_up, w_down):
    tokens, feature_width = stash.shape
    hidden = w_down.shape[2]
    experts = lax.axis_size(ROW_AXES)
    dp_count = lax.axis_size(COLUMN_AXES)
    capacity = min(tokens, 7 * tokens // (2 * experts))
    first, second = dispatch_masks(route_ids, experts, capacity)
    picks = (first | second).astype(jnp.bfloat16)
    slots = jnp.concatenate([first, second], axis=1).astype(jnp.bfloat16)
    sent_x = jnp.dot(picks, dequantize(stash, scales), preferred_element_type=jnp.float32).astype(jnp.bfloat16)
    weight_in = w_gate_up[0]
    features = exchange(sent_x, experts, capacity)
    zs = lax.axis_size("z")
    all_ids = lax.all_gather(route_ids, "z", axis=0, tiled=True)
    weights = plane_weights(w_down[0])
    slot_hidden = hidden_gradient(out_grad, all_ids, gates, weights, zs).reshape(2 * tokens, hidden)
    sent_hidden = jnp.dot(slots, slot_hidden, preferred_element_type=jnp.float32).astype(jnp.bfloat16)
    back_hidden = exchange(sent_hidden, experts, capacity).astype(jnp.float32)
    gate_up = jnp.dot(features, weight_in, preferred_element_type=jnp.float32)
    hidden_grad = gated_backward(gate_up, back_hidden)
    slot_grads = lax.dot_general(
        hidden_grad, weight_in, (((1,), (1,)), ((), ())), preferred_element_type=jnp.float32
    ).astype(jnp.bfloat16)
    returned = exchange(slot_grads, experts, capacity)
    input_grad = lax.dot_general(
        picks, returned, (((0,), (0,)), ((), ())), preferred_element_type=jnp.float32
    ).astype(jnp.bfloat16)
    local_rows = feature_width // dp_count
    partial_grad = lax.dot_general(
        features, hidden_grad, (((0,), (0,)), ((), ())), preferred_element_type=jnp.float32
    ).astype(jnp.bfloat16)
    grad_gate_up = reduce_rows(partial_grad, dp_count, 2).reshape(1, local_rows, 2 * hidden)
    return (input_grad, grad_gate_up)


def solution(mesh):
    dp_count, experts = mesh.devices.shape
    split = Mesh(
        mesh.devices.reshape(dp_count // 4, 2, 2, 2, experts // 2), COLUMN_AXES + ROW_AXES
    )
    tokens = P(COLUMN_AXES + ROW_AXES, None)
    placed = (tokens, tokens, tokens, tokens, tokens, P(ROW_AXES, None, None), P(ROW_AXES, COLUMN_AXES, None))
    return jax.shard_map(
        on_device,
        mesh=split,
        in_specs=placed,
        out_specs=(tokens, P(ROW_AXES, COLUMN_AXES, None)),
        check_vma=False,
    )
```

time: 272 us -> 225 us (0.83)
  waiting for transfers between devices: 57.9 us -> 13.1 us
  Pallas kernels: 148 us -> 115 us
  blocking collectives: 0 us -> 29.1 us
  matrix products: 41.3 us -> 31.7 us
  starting transfers between devices: 19.6 us -> 27.5 us
    all_to_all x3 -> x4, waiting for transfers between devices: 57.9 us -> 13.1 us  [the longest x1 13.1 us: plane_weights(): lax.all_to_all(copies, ('xlo',) + ROW_AXES, split_axis=0, concat_axis=0,...]
    all_gather x0 -> x1, blocking collectives: none -> 29.1 us  [on_device(): all_ids = lax.all_gather(route_ids, 'z', axis=0, tiled=True)]
    pallas_call x1, Pallas kernels: 87.9 us -> 59.4 us  [hidden_gradient(): pl.pallas_call(functools.partial(relay_kernel, zs), out_shape=jax.ShapeDt...]
    dot_general x2 -> x1, matrix products: 9.22 us -> 0.92 us  [on_device(): jnp.dot(slots, slot_hidden, preferred_element_type=jnp.float32)]
    all_to_all x3 -> x4, starting transfers between devices: 19.6 us -> 27.5 us  [the longest x3 20.1 us: exchange(): lax.all_to_all(rows.reshape(experts, capacity, width), ROW_AXES, split_ax...]
    pallas_call x1, Pallas kernels: 59.9 us -> 55.4 us  [reduce_rows(): pl.pallas_call(functools.partial(reduce_kernel, zs, subs), out_shape=jax....]
  transfers between devices with their start and end apart: 3 -> 4, of which waited for: 1 -> 1; matrix products, arithmetic and copies ran while one was open for 6% -> 10% of each run, Pallas kernels for 54% -> 51%
where the time goes in v1:
time: 225 us; the launch traced here: 224 us
  Pallas kernels  115 us (51%)
  matrix products  31.7 us (14%)
  blocking collectives  29.1 us (13%)
  starting transfers between devices  27.5 us (12%)
  waiting for transfers between devices  13.1 us (6%)
  local copies, waits for them, and re-layouts  5.99 us (3%)
    pallas_call x1, Pallas kernels, hidden_gradient(): pl.pallas_call(functools.partial(relay_kernel, zs), out_shape=jax.ShapeDt...  59.4 us
    pallas_call x1, Pallas kernels, reduce_rows(): pl.pallas_call(functools.partial(reduce_kernel, zs, subs), out_shape=jax....  55.4 us
    all_gather x1, blocking collectives, on_device(): all_ids = lax.all_gather(route_ids, 'z', axis=0, tiled=True)  29.1 us
    all_to_all x3, starting transfers between devices, exchange(): lax.all_to_all(rows.reshape(experts, capacity, width), ROW_AXES, split_ax...  20.1 us
    all_to_all x1, waiting for transfers between devices, plane_weights(): lax.all_to_all(copies, ('xlo',) + ROW_AXES, split_axis=0, concat_axis=0,...  13.1 us
    dot_general x1, matrix products, on_device(): lax.dot_general(hidden_grad, weight_in, (((1,), (1,)), ((), ())), preferr...  8.36 us
    all_to_all x1, starting transfers between devices, plane_weights(): lax.all_to_all(copies, ('xlo',) + ROW_AXES, split_axis=0, concat_axis=0,...  7.45 us
    dot_general x1, matrix products, on_device(): gate_up = jnp.dot(features, weight_in, preferred_element_type=jnp.float32)  6.8 us
  transfers between devices with their start and end apart: 4, of which 1 were waited for; matrix products, arithmetic and copies ran while one was open for 10% of the time, Pallas kernels for 51%

profile of v1, /device:TPU:4, one launch (start us, length us, event | category | flops | bytes accessed | tf_op | source)
XLA Modules:
  0.0 224.0 jit_solution(3820034704576192913)
XLA Ops:
  0.6 2.3 %broadcast_in_dim.10 = bf16[16,192,256]{2,1,0:T(8,128)(2,1)} broadcast(bf16[192,256]{1,0:T(8,128)(2,1)} %bitcast.40), dimensions={1,2} | broadcast | bytes 1671168 | tf_op jit(solution)/shard_map/broadcast_in_dim | solution.py:192
  2.9 7.5 %all-to-all-start = ((bf16[16,192,256]{2,1,0:T(8,128)(2,1)}), bf16[16,192,256]{2,1,0:T(8,128)(2,1)S(1)}, u32[]{:S(2)}, u32[]{:S(2)}) async-start(bf16[16,192,256]{2,1,0:T(8,128)(2,1)} %broadcast_in_dim.10), calls=%async_computation | async-start | bytes 3145728 | tf_op jit(solution)/shard_map/all_to_all | solution.py:193
  10.4 0.8 copy.24
  11.2 0.1 eq.46
  11.3 0.2 fusion.5
  11.5 0.1 convert_element_type.44
  11.7 0.8 copy.28
  12.6 0.7 multiply_add_fusion
  13.3 0.9 mul.38
  14.1 4.2 %convolution_convert_fusion.2 = bf16[448,6144]{1,0:T(8,128)(2,1)} fusion(f32[16,8,48,128]{3,2,1,0:T(8,128)S(1)} %bitcast.38, bf16[128,6144]{1,0:T(8,128)(2,1)S(1)} %copy-done.1, s32[128]{0:T(128)S(1)} %get-tuple-element.5, s32[128]{0:T(128)S(1)} %get-tuple-element.4), kind=kOutput, calls=%fused_computation.2 | convolution fusion | flops 709926912 | bytes 10224640 | tf_op jit(solution)/shard_map/dot_general | solution.py:379
  18.3 13.1 %all-to-all-done = bf16[16,192,256]{2,1,0:T(8,128)(2,1)S(1)} async-done(((bf16[16,192,256]{2,1,0:T(8,128)(2,1)}), bf16[16,192,256]{2,1,0:T(8,128)(2,1)S(1)}, u32[]{:S(2)}, u32[]{:S(2)}) %all-to-all-start) | async-done | bytes 1572896 | tf_op jit(solution)/shard_map/all_to_all | solution.py:193
  31.4 5.6 %all-to-all-start.2 = ((bf16[8,56,6144]{2,1,0:T(8,128)(2,1)}), bf16[8,56,6144]{2,1,0:T(8,128)(2,1)}, u32[]{:S(2)}, u32[]{:S(2)}) async-start(bf16[8,56,6144]{2,1,0:T(8,128)(2,1)} %bitcast.37), calls=%async_computation.2 | async-start | bytes 11010048 | tf_op jit(solution)/shard_map/all_to_all | solution.py:183
  37.1 29.1 %all_gather.3.ids_ref = s32[1024,2]{1,0:T(8,128)S(1)} all-gather(s32[128,2]{1,0:T(8,128)S(1)} %copy.24), channel_id=1, replica_groups=mesh['z'=8,'xlo'=2,'core'=2,'xhi'=2,'y'=4] {'z'}, dimensions={0}, use_global_device_ids=true | all-gather | bytes 9216 | tf_op jit(solution)/shard_map/all_gather | solution.py:383
  66.4 59.4 %relay_hidden.1 = bf16[2,128,256]{2,1,0:T(8,128)(2,1)S(1)} custom-call(bf16[128,6144]{1,0:T(8,128)(2,1)S(1)} %copy-done, s32[1024,2]{1,0:T(8,128)S(1)} %all_gather.3.ids_ref, f32[128,2]{1,0:T(8,128)S(1)} %copy.27.gate_ref, bf16[2,8,192,256]{3,2,1,0:T(8,128)(2,1)S(1)} %bitcast.33), custom_call_target="tpu_custom_call" | custom-call | flops 40000000000 | bytes 7000000 | tf_op jit(solution)/shard_map/relay_hidden/pallas_call | solution.py:342
  125.8 0.9 convolution_convert_fusion.4
  126.7 7.2 %all-to-all-start.1 = ((bf16[8,56,256]{2,1,0:T(8,128)(2,1)}), bf16[8,56,256]{2,1,0:T(8,128)(2,1)S(1)}, u32[]{:S(2)}, u32[]{:S(2)}) async-start(bf16[8,56,256]{2,1,0:T(8,128)(2,1)} %bitcast.5), calls=%async_computation.1 | async-start | bytes 458752 | tf_op jit(solution)/shard_map/all_to_all | solution.py:183
  133.9 6.8 %fusion.1 = f32[448,512]{1,0:T(8,128)S(1)} fusion(bf16[448,6144]{1,0:T(8,128)(2,1)} %bitcast.8, bf16[1,6144,512]{2,1,0:T(8,128)(2,1)} %param.12), kind=kOutput, calls=%fused_computation.5 | convolution fusion | flops 2818572288 | bytes 12713984 | tf_op jit(solution)/shard_map/dot_general | solution.py:388
  140.7 0.2 fusion.8
  140.9 8.4 %convolution_convert_fusion.1 = bf16[448,6144]{1,0:T(8,128)(2,1)} fusion(bf16[1,6144,512]{2,1,0:T(8,128)(2,1)} %param.12, bf16[448,256]{1,0:T(8,128)(2,1)S(1)} %get-tuple-element.3, bf16[448,256]{1,0:T(8,128)(2,1)S(1)} %get-tuple-element.2), kind=kOutput, calls=%fused_computation.1 | convolution fusion | flops 2822242304 | bytes 12255232 | tf_op jit(solution)/shard_map/dot_general | solution.py:390
  149.3 7.2 %all-to-all-start.3 = ((bf16[8,56,6144]{2,1,0:T(8,128)(2,1)}), bf16[8,56,6144]{2,1,0:T(8,128)(2,1)}, u32[]{:S(2)}, u32[]{:S(2)}) async-start(bf16[8,56,6144]{2,1,0:T(8,128)(2,1)} %bitcast.39), calls=%async_computation.3 | async-start | bytes 11010048 | tf_op jit(solution)/shard_map/all_to_all | solution.py:183
  156.5 6.5 %convolution_convert_fusion = bf16[6144,512]{1,0:T(8,128)(2,1)S(1)} fusion(bf16[448,6144]{1,0:T(8,128)(2,1)} %bitcast.8, bf16[448,256]{1,0:T(8,128)(2,1)S(1)} %get-tuple-element.3, bf16[448,256]{1,0:T(8,128)(2,1)S(1)} %get-tuple-element.2), kind=kOutput, calls=%fused_computation | convolution fusion | flops 2822635520 | bytes 12255232 | tf_op jit(solution)/shard_map/dot_general | solution.py:398
  163.1 55.4 %reduce_rows.1 = f32[192,512]{1,0:T(8,128)S(1)} custom-call(bf16[32,192,512]{2,1,0:T(8,128)(2,1)S(1)} %bitcast.35), custom_call_target="tpu_custom_call" | custom-call | flops 40000000000 | bytes 7000000 | tf_op jit(solution)/shard_map/reduce_rows/pallas_call | solution.py:120
  218.5 4.7 %convolution_convert_fusion.3 = bf16[128,6144]{1,0:T(8,128)(2,1)} fusion(bf16[448,6144]{1,0:T(8,128)(2,1)} %bitcast.12, s32[128]{0:T(128)S(1)} %get-tuple-element.5, s32[128]{0:T(128)S(1)} %get-tuple-element.4), kind=kOutput, calls=%fused_computation.3 | convolution fusion | flops 705601536 | bytes 7078912 | tf_op jit(solution)/shard_map/dot_general | solution.py:394
  223.2 0.7 copy.37
  (14 shorter events, 0.3 us)
Async XLA Ops:
  0.6 13.5 %copy-start.1 = (bf16[128,6144]{1,0:T(8,128)(2,1)S(1)}, bf16[128,6144]{1,0:T(8,128)(2,1)}, u32[]{:S(2)}) copy-start(bf16[128,6144]{1,0:T(8,128)(2,1)} %param.7) | copy-start | bytes 4718596
  2.9 28.4 %all-to-all-start = ((bf16[16,192,256]{2,1,0:T(8,128)(2,1)}), bf16[16,192,256]{2,1,0:T(8,128)(2,1)S(1)}, u32[]{:S(2)}, u32[]{:S(2)}) async-start(bf16[16,192,256]{2,1,0:T(8,128)(2,1)} %broadcast_in_dim.10), calls=%async_computation | async-start | bytes 3145728 | tf_op jit(solution)/shard_map/all_to_all | solution.py:193
  31.4 5.6 %copy-start.2 = (f32[128,2]{0,1:T(2,128)S(1)}, f32[128,2]{0,1:T(2,128)}, u32[]{:S(2)}) copy-start(f32[128,2]{0,1:T(2,128)} %param.11) | copy-start | bytes 3076
  31.4 34.9 %copy-start = (bf16[128,6144]{1,0:T(8,128)(2,1)S(1)}, bf16[128,6144]{1,0:T(8,128)(2,1)}, u32[]{:S(2)}) copy-start(bf16[128,6144]{1,0:T(8,128)(2,1)} %grad_ref.1) | copy-start | bytes 4718596
  31.4 95.3 %all-to-all-start.2 = ((bf16[8,56,6144]{2,1,0:T(8,128)(2,1)}), bf16[8,56,6144]{2,1,0:T(8,128)(2,1)}, u32[]{:S(2)}, u32[]{:S(2)}) async-start(bf16[8,56,6144]{2,1,0:T(8,128)(2,1)} %bitcast.37), calls=%async_computation.2 | async-start | bytes 11010048 | tf_op jit(solution)/shard_map/all_to_all | solution.py:183
  126.7 14.0 %all-to-all-start.1 = ((bf16[8,56,256]{2,1,0:T(8,128)(2,1)}), bf16[8,56,256]{2,1,0:T(8,128)(2,1)S(1)}, u32[]{:S(2)}, u32[]{:S(2)}) async-start(bf16[8,56,256]{2,1,0:T(8,128)(2,1)} %bitcast.5), calls=%async_computation.1 | async-start | bytes 458752 | tf_op jit(solution)/shard_map/all_to_all | solution.py:183
  149.3 69.2 %all-to-all-start.3 = ((bf16[8,56,6144]{2,1,0:T(8,128)(2,1)}), bf16[8,56,6144]{2,1,0:T(8,128)(2,1)}, u32[]{:S(2)}, u32[]{:S(2)}) async-start(bf16[8,56,6144]{2,1,0:T(8,128)(2,1)} %bitcast.39), calls=%async_computation.3 | async-start | bytes 11010048 | tf_op jit(solution)/shard_map/all_to_all | solution.py:183

commit v2 on v1

--- a/solution.py
+++ b/solution.py
@@ -142,7 +142,7 @@
     )(part.reshape(dp_count, rows, width))
 
 
-def dispatch_masks(route_ids, experts, capacity):
+def dispatch_masks(route_ids, experts, capacity, stride):
     tokens = route_ids.shape[0]
     flat_ids = route_ids.reshape(-1)
     slot_total = flat_ids.shape[0]
@@ -151,11 +151,15 @@
     before = (order[:, None] > order[None, :]).astype(jnp.bfloat16)
     earlier = jnp.dot(before, onehot.astype(jnp.bfloat16), preferred_element_type=jnp.float32)
     ranking = jnp.sum(jnp.where(onehot, earlier, 0.0), axis=1).astype(jnp.int32)
-    destination = (flat_ids * capacity + ranking).reshape(tokens, 2)
-    rows = jnp.arange(experts * capacity, dtype=jnp.int32)
-    first = rows[:, None] == destination[:, 0][None, :]
-    second = rows[:, None] == destination[:, 1][None, :]
-    return first, second
+
+    def match(pitch):
+        target = (flat_ids * pitch + ranking).reshape(tokens, 2)
+        rows = jnp.arange(experts * pitch, dtype=jnp.int32)[:, None]
+        return rows == target[:, 0][None, :], rows == target[:, 1][None, :]
+
+    first, second = match(capacity)
+    slots = jnp.concatenate(match(stride), axis=1).astype(jnp.bfloat16)
+    return (first | second).astype(jnp.bfloat16), slots
 
 
 def dequantize(stash_rows, scale_rows):
@@ -194,12 +198,23 @@
     return mine.reshape((planes, experts) + w_down.shape)
 
 
-def relay_kernel(zs, grad_ref, ids_ref, gate_ref, weight_ref, out_ref,
-                 slice_ref, wide_ref, pick_ref, stage_ref, back_ref,
+def relay_kernel(zs, sent_ref, grad_ref, ids_in_ref, gate_ref, weight_ref, slots_ref, rows_ref, out_ref,
+                 pass_ref, rows_send, rows_recv, pass_sem, ids_ref, ids_send, ids_recv,
+                 tail_ref, tail_send, tail_recv, tail_sem, slice_ref, wide_ref, pick_ref, stage_ref, back_ref,
                  own_sem, slice_send, slice_recv, weight_sem, weight_send, weight_recv, back_send, back_recv):
     z, xlo, core = ring_place()
-    tokens = out_ref.shape[1]
+    tokens = slice_ref.shape[1]
     depth = slice_ref.shape[2]
+    experts_out = sent_ref.shape[0]
+    mine = lax.axis_index("xhi") * (experts_out // 2) + lax.axis_index("y")
+
+    def row_of(shift):
+        return lax.rem(mine + shift, experts_out)
+
+    def row_place(shift):
+        row = row_of(shift)
+        return {"xhi": row // (experts_out // 2), "y": lax.rem(row, experts_out // 2)}
+
     experts = weight_ref.shape[1]
     rows = weight_ref.shape[2]
     half = zs // 2
@@ -215,7 +230,73 @@
     def mirror(slot):
         return slot if slot >= zs - 2 else slot ^ 1
 
-    greet([place(peer(offset), xlo, core) for offset in offsets[:-1]] + [twin])
+    greet(
+        [place(peer(offset), xlo, core) for offset in offsets[:-1]]
+        + [twin]
+        + [row_place(shift) for shift in range(1, experts_out)]
+    )
+
+    def rows_copy(shift):
+        return pltpu.make_async_remote_copy(
+            src_ref=sent_ref.at[row_of(shift)],
+            dst_ref=rows_ref.at[mine],
+            send_sem=rows_send.at[shift - 1],
+            recv_sem=rows_recv.at[shift - 1],
+            device_id=row_place(shift),
+            device_id_type=MESH,
+        )
+
+    def rows_arrival(shift):
+        source = row_of(experts_out - shift)
+        return pltpu.make_async_remote_copy(
+            src_ref=sent_ref.at[source],
+            dst_ref=rows_ref.at[source],
+            send_sem=rows_send.at[shift - 1],
+            recv_sem=rows_recv.at[shift - 1],
+            device_id=twin,
+            device_id_type=MESH,
+        )
+
+    def tail_copy(shift):
+        return pltpu.make_async_remote_copy(
+            src_ref=tail_ref.at[row_of(shift)],
+            dst_ref=out_ref.at[mine],
+            send_sem=tail_send.at[shift - 1],
+            recv_sem=tail_recv.at[shift - 1],
+            device_id=row_place(shift),
+            device_id_type=MESH,
+        )
+
+    def tail_arrival(shift):
+        source = row_of(experts_out - shift)
+        return pltpu.make_async_remote_copy(
+            src_ref=tail_ref.at[source],
+            dst_ref=out_ref.at[source],
+            send_sem=tail_send.at[shift - 1],
+            recv_sem=tail_recv.at[shift - 1],
+            device_id=twin,
+            device_id_type=MESH,
+        )
+
+    def ids_copy(slot):
+        return pltpu.make_async_remote_copy(
+            src_ref=ids_in_ref,
+            dst_ref=ids_ref.at[mirror(slot)],
+            send_sem=ids_send.at[slot],
+            recv_sem=ids_recv.at[mirror(slot)],
+            device_id=place(peer(offsets[slot]), xlo, core),
+            device_id_type=MESH,
+        )
+
+    def ids_arrival(slot):
+        return pltpu.make_async_remote_copy(
+            src_ref=ids_ref.at[slot],
+            dst_ref=ids_ref.at[slot],
+            send_sem=ids_send.at[slot],
+            recv_sem=ids_recv.at[slot],
+            device_id=twin,
+            device_id_type=MESH,
+        )
 
     def columns(offset):
         return pl.ds(pl.multiple_of(peer(offset) * depth, depth), depth)
@@ -286,20 +367,31 @@
     keeps = [pltpu.make_async_copy(grad_ref.at[:, columns(0)], slice_ref.at[zs - 1], own_sem)]
     for plane in range(2):
         keeps.append(pltpu.make_async_copy(weight_ref.at[plane], weight_rows(plane, core), weight_sem.at[plane]))
+    for shift in range(1, experts_out):
+        rows_copy(shift).start()
+    for slot in range(zs - 1):
+        ids_copy(slot).start()
     for slot in range(zs - 1):
         slice_copy(slot).start()
     for plane in range(2):
         weight_copy(plane).start()
+    pass_in = pltpu.make_async_copy(sent_ref.at[mine], pass_ref, pass_sem)
+    pass_out = pltpu.make_async_copy(pass_ref, rows_ref.at[mine], pass_sem)
+    pass_in.start()
+    ids_ref[zs - 1] = ids_in_ref[...]
     for keep in keeps:
         keep.start()
     for keep in keeps:
         keep.wait()
+    pass_in.wait()
+    pass_out.start()
     for plane in range(2):
         weight_arrival(plane).wait_recv()
     for pair in range(half):
         for side in range(2):
             slot = 2 * pair + side
             if slot < zs - 1:
+                ids_arrival(slot).wait_recv()
                 slice_arrival(slot).wait_recv()
         pick_ref[...] = jnp.zeros_like(pick_ref)
 
@@ -308,9 +400,8 @@
             for side in range(2):
                 slot = 2 * pair + side
                 dense = jnp.dot(slice_ref[slot], wide, preferred_element_type=jnp.float32)
-                first_row = pl.multiple_of(peer(offsets[slot]) * tokens, tokens)
                 for k in range(2):
-                    chosen = ids_ref[pl.ds(first_row, tokens), k : k + 1] == e
+                    chosen = ids_ref[slot, :, k : k + 1] == e
                     pick_ref[side, k] = jnp.where(chosen, dense, pick_ref[side, k])
             return carry
 
@@ -324,47 +415,79 @@
     for slot in range(zs - 1):
         back_arrival(slot).wait_recv()
         total = total + back_ref[slot].astype(jnp.float32)
-    for k in range(2):
-        out_ref[k] = (total[k] * gate_ref[:, k : k + 1]).astype(out_ref.dtype)
+    weighted = [(total[k] * gate_ref[:, k : k + 1]).astype(tail_ref.dtype) for k in range(2)]
+    placed = jnp.dot(slots_ref[...], jnp.concatenate(weighted, axis=0), preferred_element_type=jnp.float32)
+    tail_ref[...] = placed.astype(tail_ref.dtype).reshape(tail_ref.shape)
+    for shift in range(1, experts_out):
+        tail_copy(shift).start()
+    keep_tail = pltpu.make_async_copy(tail_ref.at[mine], out_ref.at[mine], tail_sem)
+    keep_tail.start()
+    for shift in range(1, experts_out):
+        rows_arrival(shift).wait_recv()
     for slot in range(zs - 1):
+        ids_copy(slot).wait_send()
         slice_copy(slot).wait_send()
         back_copy(slot).wait_send()
     for plane in range(2):
         weight_copy(plane).wait_send()
-
-
-def hidden_gradient(out_grad, all_ids, gates, weights, zs):
+    pass_out.wait()
+    for shift in range(1, experts_out):
+        tail_arrival(shift).wait_recv()
+        rows_copy(shift).wait_send()
+        tail_copy(shift).wait_send()
+    keep_tail.wait()
+
+
+def relay(sent_x, out_grad, route_ids, gates, weights, slots, zs):
     tokens, feature_width = out_grad.shape
     planes, experts, rows, hidden = weights.shape
     depth = feature_width // zs
+    tail_rows = slots.shape[0] // experts
     kind = out_grad.dtype
     vmem = pl.BlockSpec(memory_space=pltpu.VMEM)
+    anywhere = pl.BlockSpec(memory_space=pl.ANY)
+    pairs = pltpu.SemaphoreType.DMA((zs - 1,))
+    others = pltpu.SemaphoreType.DMA((experts - 1,))
     return pl.pallas_call(
         functools.partial(relay_kernel, zs),
-        out_shape=jax.ShapeDtypeStruct((2, tokens, hidden), kind),
-        in_specs=[pl.BlockSpec(memory_space=pl.ANY), vmem, vmem, pl.BlockSpec(memory_space=pl.ANY)],
-        out_specs=vmem,
+        out_shape=(
+            jax.ShapeDtypeStruct(sent_x.shape, kind),
+            jax.ShapeDtypeStruct((experts, tail_rows, hidden), kind),
+        ),
+        in_specs=[anywhere, anywhere, vmem, vmem, anywhere, vmem],
+        out_specs=(anywhere, anywhere),
         scratch_shapes=[
+            pltpu.VMEM(sent_x.shape[1:], kind),
+            others,
+            others,
+            pltpu.SemaphoreType.DMA,
+            pltpu.VMEM((zs,) + route_ids.shape, route_ids.dtype),
+            pairs,
+            pairs,
+            pltpu.VMEM((experts, tail_rows, hidden), kind),
+            others,
+            others,
+            pltpu.SemaphoreType.DMA,
             pltpu.VMEM((zs, tokens, depth), kind),
             pltpu.VMEM((experts, 2 * planes * rows, hidden), kind),
             pltpu.VMEM((2, 2, tokens, hidden), jnp.float32),
             pltpu.VMEM((zs, 2, tokens, hidden), kind),
             pltpu.VMEM((zs - 1, 2, tokens, hidden), kind),
             pltpu.SemaphoreType.DMA,
-            pltpu.SemaphoreType.DMA((zs - 1,)),
-            pltpu.SemaphoreType.DMA((zs - 1,)),
+            pairs,
+            pairs,
             pltpu.SemaphoreType.DMA((2,)),
             pltpu.SemaphoreType.DMA((2,)),
             pltpu.SemaphoreType.DMA((2,)),
-            pltpu.SemaphoreType.DMA((zs - 1,)),
-            pltpu.SemaphoreType.DMA((zs - 1,)),
+            pairs,
+            pairs,
         ],
         compiler_params=pltpu.CompilerParams(
             collective_id=1, has_side_effects=True, vmem_limit_bytes=24 * 1024 * 1024
         ),
         cost_estimate=pl.CostEstimate(flops=40_000_000_000, bytes_accessed=7_000_000, transcendentals=0),
-        name="relay_hidden",
-    )(out_grad, all_ids, gates, weights)
+        name="relay",
+    )(sent_x, out_grad, route_ids, gates, weights, slots)
 
 
 def on_device(stash, scales, out_grad, route_ids, gates, w_gate_up, w_down):
@@ -373,18 +496,17 @@
     experts = lax.axis_size(ROW_AXES)
     dp_count = lax.axis_size(COLUMN_AXES)
     capacity = min(tokens, 7 * tokens // (2 * experts))
-    first, second = dispatch_masks(route_ids, experts, capacity)
-    picks = (first | second).astype(jnp.bfloat16)
-    slots = jnp.concatenate([first, second], axis=1).astype(jnp.bfloat16)
+    stride = -(-capacity // 16) * 16
+    picks, slots = dispatch_masks(route_ids, experts, capacity, stride)
     sent_x = jnp.dot(picks, dequantize(stash, scales), preferred_element_type=jnp.float32).astype(jnp.bfloat16)
     weight_in = w_gate_up[0]
-    features = exchange(sent_x, experts, capacity)
     zs = lax.axis_size("z")
-    all_ids = lax.all_gather(route_ids, "z", axis=0, tiled=True)
     weights = plane_weights(w_down[0])
-    slot_hidden = hidden_gradient(out_grad, all_ids, gates, weights, zs).reshape(2 * tokens, hidden)
-    sent_hidden = jnp.dot(slots, slot_hidden, preferred_element_type=jnp.float32).astype(jnp.bfloat16)
-    back_hidden = exchange(sent_hidden, experts, capacity).astype(jnp.float32)
+    got_x, got_hidden = relay(
+        sent_x.reshape(experts, capacity, feature_width), out_grad, route_ids, gates, weights, slots, zs
+    )
+    features = got_x.reshape(experts * capacity, feature_width)
+    back_hidden = got_hidden[:, :capacity].reshape(experts * capacity, hidden).astype(jnp.float32)
     gate_up = jnp.dot(features, weight_in, preferred_element_type=jnp.float32)
     hidden_grad = gated_backward(gate_up, back_hidden)
     slot_grads = lax.dot_general(

time: 225 us -> 220 us (0.978)
  Pallas kernels: 115 us -> 151 us
  blocking collectives: 29.1 us -> 0 us
  starting transfers between devices: 27.5 us -> 13.9 us
  local copies, waits for them, and re-layouts: 5.99 us -> 9.13 us
  waiting for transfers between devices: 13.1 us -> 10.6 us
    pallas_call x1, Pallas kernels: 59.4 us -> 91.9 us  [relay(): pl.pallas_call(functools.partial(relay_kernel, zs), out_shape=(jax.ShapeD...]
    all_gather x1 -> x0, blocking collectives: 29.1 us -> none  [on_device(): all_ids = lax.all_gather(route_ids, 'z', axis=0, tiled=True)]
    all_to_all x3 -> x1, starting transfers between devices: 20.1 us -> 6.47 us  [exchange(): lax.all_to_all(rows.reshape(experts, capacity, width), ROW_AXES, split_ax...]
    pallas_call x1, Pallas kernels: 55.4 us -> 58.9 us  [reduce_rows(): pl.pallas_call(functools.partial(reduce_kernel, zs, subs), out_shape=jax....]
    unnamed x9, local copies, waits for them, and re-layouts: 1.65 us -> 4.89 us
    all_to_all x1, waiting for transfers between devices: 13.1 us -> 10.6 us  [plane_weights(): lax.all_to_all(copies, ('xlo',) + ROW_AXES, split_axis=0, concat_axis=0,...]
  transfers between devices with their start and end apart: 4 -> 2, of which waited for: 1 -> 1; matrix products, arithmetic and copies ran while one was open for 10% -> 8% of each run, Pallas kernels for 51% -> 27%
where the time goes in v2:
time: 220 us; the launch traced here: 219 us
  Pallas kernels  151 us (69%)
  matrix products  32.8 us (15%)
  starting transfers between devices  13.9 us (6%)
  waiting for transfers between devices  10.6 us (5%)
  local copies, waits for them, and re-layouts  9.13 us (4%)
    pallas_call x1, Pallas kernels, relay(): pl.pallas_call(functools.partial(relay_kernel, zs), out_shape=(jax.ShapeD...  91.9 us
    pallas_call x1, Pallas kernels, reduce_rows(): pl.pallas_call(functools.partial(reduce_kernel, zs, subs), out_shape=jax....  58.9 us
    all_to_all x1, waiting for transfers between devices, plane_weights(): lax.all_to_all(copies, ('xlo',) + ROW_AXES, split_axis=0, concat_axis=0,...  10.6 us
    dot_general x1, matrix products, on_device(): lax.dot_general(hidden_grad, weight_in, (((1,), (1,)), ((), ())), preferr...  8.46 us
    all_to_all x1, starting transfers between devices, plane_weights(): lax.all_to_all(copies, ('xlo',) + ROW_AXES, split_axis=0, concat_axis=0,...  7.45 us
    dot_general x1, matrix products, on_device(): gate_up = jnp.dot(features, weight_in, preferred_element_type=jnp.float32)  7.19 us
    dot_general x1, matrix products, on_device(): lax.dot_general(features, hidden_grad, (((0,), (0,)), ((), ())), preferre...  6.51 us
    all_to_all x1, starting transfers between devices, exchange(): lax.all_to_all(rows.reshape(experts, capacity, width), ROW_AXES, split_ax...  6.47 us
  transfers between devices with their start and end apart: 2, of which 1 were waited for; matrix products, arithmetic and copies ran while one was open for 8% of the time, Pallas kernels for 27%

profile of v2, /device:TPU:4, one launch (start us, length us, event | category | flops | bytes accessed | tf_op | source)
XLA Modules:
  0.0 219.1 jit_solution(8802826035917748698)
XLA Ops:
  0.6 2.2 broadcast_in_dim.10
  2.8 7.5 %all-to-all-start = ((bf16[16,192,256]{2,1,0:T(8,128)(2,1)}), bf16[16,192,256]{2,1,0:T(8,128)(2,1)S(1)}, u32[]{:S(2)}, u32[]{:S(2)}) async-start(bf16[16,192,256]{2,1,0:T(8,128)(2,1)} %broadcast_in_dim.10), calls=%async_computation | async-start | bytes 3145728 | tf_op jit(solution)/shard_map/all_to_all | solution.py:197
  10.3 0.8 copy.28.ids_in_ref
  11.1 0.1 eq.76
  11.2 0.2 fusion.5
  11.4 0.1 convert_element_type.44
  11.6 0.1 copy.29
  11.6 0.8 copy.30
  12.4 0.8 copy.33.gate_ref
  13.2 0.7 multiply_add_fusion
  14.0 0.1 add_convert_fusion.slots_ref
  14.1 0.9 mul.45
  15.0 5.7 %convolution_convert_fusion.2 = bf16[448,6144]{1,0:T(8,128)(2,1)} fusion(f32[16,8,48,128]{3,2,1,0:T(8,128)S(1)} %bitcast.40, bf16[128,6144]{1,0:T(8,128)(2,1)} %param.7, s32[128]{0:T(128)S(1)} %get-tuple-element.14, s32[128]{0:T(128)S(1)} %get-tuple-element.15), kind=kOutput, calls=%fused_computation.2 | convolution fusion | flops 709926912 | bytes 10224640 | tf_op jit(solution)/shard_map/dot_general | solution.py:501
  20.6 10.6 %all-to-all-done = bf16[16,192,256]{2,1,0:T(8,128)(2,1)S(1)} async-done(((bf16[16,192,256]{2,1,0:T(8,128)(2,1)}), bf16[16,192,256]{2,1,0:T(8,128)(2,1)S(1)}, u32[]{:S(2)}, u32[]{:S(2)}) %all-to-all-start) | async-done | bytes 1572896 | tf_op jit(solution)/shard_map/all_to_all | solution.py:197
  31.3 2.6 %copy-done = bf16[448,6144]{1,0:T(8,128)(2,1)S(1)} copy-done((bf16[448,6144]{1,0:T(8,128)(2,1)S(1)}, bf16[448,6144]{1,0:T(8,128)(2,1)}, u32[]{:S(2)}) %copy-start) | copy-done | bytes 5505048
  33.8 91.9 %relay.1 = (bf16[8,56,6144]{2,1,0:T(8,128)(2,1)S(1)}, bf16[8,64,256]{2,1,0:T(8,128)(2,1)S(1)}) custom-call(bf16[8,56,6144]{2,1,0:T(8,128)(2,1)S(1)} %bitcast.34, bf16[128,6144]{1,0:T(8,128)(2,1)S(1)} %copy-done.1, s32[128,2]{1,0:T(8,128)S(1)} %copy.28.ids_in_ref, f32[128,2]{1,0:T(8,128)S(1)} %copy.33.gate_ref, bf16[2,8,192,256]{3,2,1,0:T(8,128)(2,1)S(1)} %bitcast.35, ...), custom_call_target="tpu_custom_call" | custom-call | flops 40000000000 | bytes 7000000 | tf_op jit(solution)/shard_map/relay/pallas_call | solution.py:451
  125.8 7.2 %fusion.1 = f32[448,512]{1,0:T(8,128)S(1)} fusion(bf16[448,6144]{1,0:T(8,128)(2,1)S(1)} %bitcast.38, bf16[1,6144,512]{2,1,0:T(8,128)(2,1)} %param.12), kind=kOutput, calls=%fused_computation.5 | convolution fusion | flops 2818572288 | bytes 12713984 | tf_op jit(solution)/shard_map/dot_general | solution.py:510
  133.0 0.2 fusion.8
  133.3 8.5 %convolution_convert_fusion.1 = bf16[448,6144]{1,0:T(8,128)(2,1)} fusion(bf16[1,6144,512]{2,1,0:T(8,128)(2,1)} %param.12, bf16[448,256]{1,0:T(8,128)(2,1)S(1)} %get-tuple-element.7, bf16[448,256]{1,0:T(8,128)(2,1)S(1)} %get-tuple-element.6), kind=kOutput, calls=%fused_computation.1 | convolution fusion | flops 2822242304 | bytes 12255232 | tf_op jit(solution)/shard_map/dot_general | solution.py:512
  141.7 6.5 %all-to-all-start.1 = ((bf16[8,56,6144]{2,1,0:T(8,128)(2,1)}), bf16[8,56,6144]{2,1,0:T(8,128)(2,1)}, u32[]{:S(2)}, u32[]{:S(2)}) async-start(bf16[8,56,6144]{2,1,0:T(8,128)(2,1)} %bitcast.41), calls=%async_computation.1 | async-start | bytes 11010048 | tf_op jit(solution)/shard_map/all_to_all | solution.py:187
  148.2 6.5 %convolution_convert_fusion = bf16[6144,512]{1,0:T(8,128)(2,1)S(1)} fusion(bf16[448,6144]{1,0:T(8,128)(2,1)} %bitcast.39, bf16[448,256]{1,0:T(8,128)(2,1)S(1)} %get-tuple-element.7, bf16[448,256]{1,0:T(8,128)(2,1)S(1)} %get-tuple-element.6), kind=kOutput, calls=%fused_computation | convolution fusion | flops 2822635520 | bytes 12255232 | tf_op jit(solution)/shard_map/dot_general | solution.py:520
  154.7 58.9 %reduce_rows.1 = f32[192,512]{1,0:T(8,128)S(1)} custom-call(bf16[32,192,512]{2,1,0:T(8,128)(2,1)S(1)} %bitcast.37), custom_call_target="tpu_custom_call" | custom-call | flops 40000000000 | bytes 7000000 | tf_op jit(solution)/shard_map/reduce_rows/pallas_call | solution.py:120
  213.6 4.7 %convolution_convert_fusion.3 = bf16[128,6144]{1,0:T(8,128)(2,1)} fusion(bf16[448,6144]{1,0:T(8,128)(2,1)} %bitcast.12, s32[128]{0:T(128)S(1)} %get-tuple-element.14, s32[128]{0:T(128)S(1)} %get-tuple-element.15), kind=kOutput, calls=%fused_computation.3 | convolution fusion | flops 705601536 | bytes 7078912 | tf_op jit(solution)/shard_map/dot_general | solution.py:516
  218.3 0.7 copy.38
  (11 shorter events, 0.1 us)
Async XLA Ops:
  2.8 28.4 %all-to-all-start = ((bf16[16,192,256]{2,1,0:T(8,128)(2,1)}), bf16[16,192,256]{2,1,0:T(8,128)(2,1)S(1)}, u32[]{:S(2)}, u32[]{:S(2)}) async-start(bf16[16,192,256]{2,1,0:T(8,128)(2,1)} %broadcast_in_dim.10), calls=%async_computation | async-start | bytes 3145728 | tf_op jit(solution)/shard_map/all_to_all | solution.py:197
  15.0 16.3 %copy-start.1 = (bf16[128,6144]{1,0:T(8,128)(2,1)S(1)}, bf16[128,6144]{1,0:T(8,128)(2,1)}, u32[]{:S(2)}) copy-start(bf16[128,6144]{1,0:T(8,128)(2,1)} %grad_ref.1) | copy-start | bytes 4718596
  31.3 2.6 %copy-start = (bf16[448,6144]{1,0:T(8,128)(2,1)S(1)}, bf16[448,6144]{1,0:T(8,128)(2,1)}, u32[]{:S(2)}) copy-start(bf16[448,6144]{1,0:T(8,128)(2,1)} %convolution_convert_fusion.2) | copy-start | bytes 16515076
  125.8 7.2 %copy-start.2 = (bf16[8,56,6144]{2,1,0:T(8,128)(2,1)}, bf16[8,56,6144]{2,1,0:T(8,128)(2,1)S(1)}, u32[]{:S(2)}) copy-start(bf16[8,56,6144]{2,1,0:T(8,128)(2,1)S(1)} %get-tuple-element.5) | copy-start | bytes 16515076
  141.7 71.9 %all-to-all-start.1 = ((bf16[8,56,6144]{2,1,0:T(8,128)(2,1)}), bf16[8,56,6144]{2,1,0:T(8,128)(2,1)}, u32[]{:S(2)}, u32[]{:S(2)}) async-start(bf16[8,56,6144]{2,1,0:T(8,128)(2,1)} %bitcast.41), calls=%async_computation.1 | async-start | bytes 11010048 | tf_op jit(solution)/shard_map/all_to_all | solution.py:187

commit v3 on v2

--- a/solution.py
+++ b/solution.py
@@ -198,14 +198,13 @@
     return mine.reshape((planes, experts) + w_down.shape)
 
 
-def relay_kernel(zs, sent_ref, grad_ref, ids_in_ref, gate_ref, weight_ref, slots_ref, rows_ref, out_ref,
-                 pass_ref, rows_send, rows_recv, pass_sem, ids_ref, ids_send, ids_recv,
+def relay_kernel(zs, grad_ref, ids_in_ref, gate_ref, weight_ref, slots_ref, out_ref, ids_ref, ids_send, ids_recv,
                  tail_ref, tail_send, tail_recv, tail_sem, slice_ref, wide_ref, pick_ref, stage_ref, back_ref,
                  own_sem, slice_send, slice_recv, weight_sem, weight_send, weight_recv, back_send, back_recv):
     z, xlo, core = ring_place()
     tokens = slice_ref.shape[1]
     depth = slice_ref.shape[2]
-    experts_out = sent_ref.shape[0]
+    experts_out = out_ref.shape[0]
     mine = lax.axis_index("xhi") * (experts_out // 2) + lax.axis_index("y")
 
     def row_of(shift):
@@ -236,27 +235,6 @@
         + [row_place(shift) for shift in range(1, experts_out)]
     )
 
-    def rows_copy(shift):
-        return pltpu.make_async_remote_copy(
-            src_ref=sent_ref.at[row_of(shift)],
-            dst_ref=rows_ref.at[mine],
-            send_sem=rows_send.at[shift - 1],
-            recv_sem=rows_recv.at[shift - 1],
-            device_id=row_place(shift),
-            device_id_type=MESH,
-        )
-
-    def rows_arrival(shift):
-        source = row_of(experts_out - shift)
-        return pltpu.make_async_remote_copy(
-            src_ref=sent_ref.at[source],
-            dst_ref=rows_ref.at[source],
-            send_sem=rows_send.at[shift - 1],
-            recv_sem=rows_recv.at[shift - 1],
-            device_id=twin,
-            device_id_type=MESH,
-        )
-
     def tail_copy(shift):
         return pltpu.make_async_remote_copy(
             src_ref=tail_ref.at[row_of(shift)],
@@ -367,24 +345,17 @@
     keeps = [pltpu.make_async_copy(grad_ref.at[:, columns(0)], slice_ref.at[zs - 1], own_sem)]
     for plane in range(2):
         keeps.append(pltpu.make_async_copy(weight_ref.at[plane], weight_rows(plane, core), weight_sem.at[plane]))
-    for shift in range(1, experts_out):
-        rows_copy(shift).start()
     for slot in range(zs - 1):
         ids_copy(slot).start()
     for slot in range(zs - 1):
         slice_copy(slot).start()
     for plane in range(2):
         weight_copy(plane).start()
-    pass_in = pltpu.make_async_copy(sent_ref.at[mine], pass_ref, pass_sem)
-    pass_out = pltpu.make_async_copy(pass_ref, rows_ref.at[mine], pass_sem)
-    pass_in.start()
     ids_ref[zs - 1] = ids_in_ref[...]
     for keep in keeps:
         keep.start()
     for keep in keeps:
         keep.wait()
-    pass_in.wait()
-    pass_out.start()
     for plane in range(2):
         weight_arrival(plane).wait_recv()
     for pair in range(half):
@@ -422,23 +393,19 @@
         tail_copy(shift).start()
     keep_tail = pltpu.make_async_copy(tail_ref.at[mine], out_ref.at[mine], tail_sem)
     keep_tail.start()
-    for shift in range(1, experts_out):
-        rows_arrival(shift).wait_recv()
     for slot in range(zs - 1):
         ids_copy(slot).wait_send()
         slice_copy(slot).wait_send()
         back_copy(slot).wait_send()
     for plane in range(2):
         weight_copy(plane).wait_send()
-    pass_out.wait()
     for shift in range(1, experts_out):
         tail_arrival(shift).wait_recv()
-        rows_copy(shift).wait_send()
         tail_copy(shift).wait_send()
     keep_tail.wait()
 
 
-def relay(sent_x, out_grad, route_ids, gates, weights, slots, zs):
+def relay(out_grad, route_ids, gates, weights, slots, zs):
     tokens, feature_width = out_grad.shape
     planes, experts, rows, hidden = weights.shape
     depth = feature_width // zs
@@ -450,17 +417,10 @@
     others = pltpu.SemaphoreType.DMA((experts - 1,))
     return pl.pallas_call(
         functools.partial(relay_kernel, zs),
-        out_shape=(
-            jax.ShapeDtypeStruct(sent_x.shape, kind),
-            jax.ShapeDtypeStruct((experts, tail_rows, hidden), kind),
-        ),
-        in_specs=[anywhere, anywhere, vmem, vmem, anywhere, vmem],
-        out_specs=(anywhere, anywhere),
+        out_shape=jax.ShapeDtypeStruct((experts, tail_rows, hidden), kind),
+        in_specs=[anywhere, vmem, vmem, anywhere, vmem],
+        out_specs=anywhere,
         scratch_shapes=[
-            pltpu.VMEM(sent_x.shape[1:], kind),
-            others,
-            others,
-            pltpu.SemaphoreType.DMA,
             pltpu.VMEM((zs,) + route_ids.shape, route_ids.dtype),
             pairs,
             pairs,
@@ -487,7 +447,7 @@
         ),
         cost_estimate=pl.CostEstimate(flops=40_000_000_000, bytes_accessed=7_000_000, transcendentals=0),
         name="relay",
-    )(sent_x, out_grad, route_ids, gates, weights, slots)
+    )(out_grad, route_ids, gates, weights, slots)
 
 
 def on_device(stash, scales, out_grad, route_ids, gates, w_gate_up, w_down):
@@ -502,10 +462,8 @@
     weight_in = w_gate_up[0]
     zs = lax.axis_size("z")
     weights = plane_weights(w_down[0])
-    got_x, got_hidden = relay(
-        sent_x.reshape(experts, capacity, feature_width), out_grad, route_ids, gates, weights, slots, zs
-    )
-    features = got_x.reshape(experts * capacity, feature_width)
+    features = exchange(sent_x, experts, capacity)
+    got_hidden = relay(out_grad, route_ids, gates, weights, slots, zs)
     back_hidden = got_hidden[:, :capacity].reshape(experts * capacity, hidden).astype(jnp.float32)
     gate_up = jnp.dot(features, weight_in, preferred_element_type=jnp.float32)
     hidden_grad = gated_backward(gate_up, back_hidden)

time: 220 us -> 212 us (0.964)
  Pallas kernels: 151 us -> 137 us
  starting transfers between devices: 13.9 us -> 21.4 us
  local copies, waits for them, and re-layouts: 9.13 us -> 6.01 us
  waiting for transfers between devices: 10.6 us -> 13 us
    pallas_call x1, Pallas kernels: 91.9 us -> 83.3 us  [relay(): pl.pallas_call(functools.partial(relay_kernel, zs), out_shape=jax.ShapeDt...]
    all_to_all x1 -> x2, starting transfers between devices: 6.47 us -> 13.9 us  [exchange(): lax.all_to_all(rows.reshape(experts, capacity, width), ROW_AXES, split_ax...]
    pallas_call x1, Pallas kernels: 58.9 us -> 53.5 us  [reduce_rows(): pl.pallas_call(functools.partial(reduce_kernel, zs, subs), out_shape=jax....]
    unnamed x9, local copies, waits for them, and re-layouts: 4.89 us -> 1.65 us
    all_to_all x1, waiting for transfers between devices: 10.6 us -> 13 us  [plane_weights(): lax.all_to_all(copies, ('xlo',) + ROW_AXES, split_axis=0, concat_axis=0,...]
  transfers between devices with their start and end apart: 2 -> 3, of which waited for: 1 -> 1; matrix products, arithmetic and copies ran while one was open for 8% -> 7% of each run, Pallas kernels for 27% -> 65%
where the time goes in v3:
time: 212 us; the launch traced here: 210 us
  Pallas kernels  137 us (65%)
  matrix products  30.8 us (15%)
  starting transfers between devices  21.4 us (10%)
  waiting for transfers between devices  13 us (6%)
  local copies, waits for them, and re-layouts  6.01 us (3%)
    pallas_call x1, Pallas kernels, relay(): pl.pallas_call(functools.partial(relay_kernel, zs), out_shape=jax.ShapeDt...  83.3 us
    pallas_call x1, Pallas kernels, reduce_rows(): pl.pallas_call(functools.partial(reduce_kernel, zs, subs), out_shape=jax....  53.5 us
    all_to_all x2, starting transfers between devices, exchange(): lax.all_to_all(rows.reshape(experts, capacity, width), ROW_AXES, split_ax...  13.9 us
    all_to_all x1, waiting for transfers between devices, plane_weights(): lax.all_to_all(copies, ('xlo',) + ROW_AXES, split_axis=0, concat_axis=0,...  13 us
    dot_general x1, matrix products, on_device(): lax.dot_general(hidden_grad, weight_in, (((1,), (1,)), ((), ())), preferr...  8.36 us
    all_to_all x1, starting transfers between devices, plane_weights(): lax.all_to_all(copies, ('xlo',) + ROW_AXES, split_axis=0, concat_axis=0,...  7.45 us
    dot_general x1, matrix products, on_device(): gate_up = jnp.dot(features, weight_in, preferred_element_type=jnp.float32)  6.81 us
    dot_general x1, matrix products, on_device(): lax.dot_general(features, hidden_grad, (((0,), (0,)), ((), ())), preferre...  6.52 us
  transfers between devices with their start and end apart: 3, of which 1 were waited for; matrix products, arithmetic and copies ran while one was open for 7% of the time, Pallas kernels for 65%

profile of v3, /device:TPU:4, one launch (start us, length us, event | category | flops | bytes accessed | tf_op | source)
XLA Modules:
  0.0 209.9 jit_solution(13049891942367281410)
XLA Ops:
  0.6 2.3 %broadcast_in_dim.10 = bf16[16,192,256]{2,1,0:T(8,128)(2,1)} broadcast(bf16[192,256]{1,0:T(8,128)(2,1)} %bitcast.40), dimensions={1,2} | broadcast | bytes 1671168 | tf_op jit(solution)/shard_map/broadcast_in_dim | solution.py:196
  2.9 7.5 %all-to-all-start = ((bf16[16,192,256]{2,1,0:T(8,128)(2,1)}), bf16[16,192,256]{2,1,0:T(8,128)(2,1)S(1)}, u32[]{:S(2)}, u32[]{:S(2)}) async-start(bf16[16,192,256]{2,1,0:T(8,128)(2,1)} %broadcast_in_dim.10), calls=%async_computation | async-start | bytes 3145728 | tf_op jit(solution)/shard_map/all_to_all | solution.py:197
  10.4 0.8 copy.28.ids_in_ref
  11.2 0.1 eq.76
  11.3 0.2 fusion.5
  11.5 0.1 convert_element_type.44
  11.7 0.1 copy.29
  11.7 0.8 copy.33
  12.6 0.7 multiply_add_fusion
  13.3 0.9 mul.47
  14.1 4.2 %convolution_convert_fusion.2 = bf16[448,6144]{1,0:T(8,128)(2,1)} fusion(f32[16,8,48,128]{3,2,1,0:T(8,128)S(1)} %bitcast.38, bf16[128,6144]{1,0:T(8,128)(2,1)S(1)} %copy-done.1, s32[128]{0:T(128)S(1)} %get-tuple-element.10, s32[128]{0:T(128)S(1)} %get-tuple-element.11), kind=kOutput, calls=%fused_computation.2 | convolution fusion | flops 709926912 | bytes 10224640 | tf_op jit(solution)/shard_map/dot_general | solution.py:461
  18.4 13.0 %all-to-all-done = bf16[16,192,256]{2,1,0:T(8,128)(2,1)S(1)} async-done(((bf16[16,192,256]{2,1,0:T(8,128)(2,1)}), bf16[16,192,256]{2,1,0:T(8,128)(2,1)S(1)}, u32[]{:S(2)}, u32[]{:S(2)}) %all-to-all-start) | async-done | bytes 1572896 | tf_op jit(solution)/shard_map/all_to_all | solution.py:197
  31.4 5.6 %all-to-all-start.1 = ((bf16[8,56,6144]{2,1,0:T(8,128)(2,1)}), bf16[8,56,6144]{2,1,0:T(8,128)(2,1)}, u32[]{:S(2)}, u32[]{:S(2)}) async-start(bf16[8,56,6144]{2,1,0:T(8,128)(2,1)} %bitcast.37), calls=%async_computation.1 | async-start | bytes 11010048 | tf_op jit(solution)/shard_map/all_to_all | solution.py:187
  37.0 0.1 copy.32.gate_ref
  37.2 0.1 add_convert_fusion.slots_ref
  37.3 83.3 %relay.1 = bf16[8,64,256]{2,1,0:T(8,128)(2,1)S(1)} custom-call(bf16[128,6144]{1,0:T(8,128)(2,1)S(1)} %copy-done, s32[128,2]{1,0:T(8,128)S(1)} %copy.28.ids_in_ref, f32[128,2]{1,0:T(8,128)S(1)} %copy.32.gate_ref, bf16[2,8,192,256]{3,2,1,0:T(8,128)(2,1)S(1)} %bitcast.34, bf16[512,256]{1,0:T(8,128)(2,1)S(1)} %add_convert_fusion.slots_ref), custom_call_target="tpu_custom_call" | custom-call | flops 40000000000 | bytes 7000000 | tf_op jit(solution)/shard_map/relay/pallas_call | solution.py:418
  120.6 6.8 %fusion.1 = f32[448,512]{1,0:T(8,128)S(1)} fusion(bf16[448,6144]{1,0:T(8,128)(2,1)} %bitcast.8, bf16[1,6144,512]{2,1,0:T(8,128)(2,1)} %param.12), kind=kOutput, calls=%fused_computation.5 | convolution fusion | flops 2818572288 | bytes 12713984 | tf_op jit(solution)/shard_map/dot_general | solution.py:468
  127.5 0.2 fusion.8
  127.7 8.4 %convolution_convert_fusion.1 = bf16[448,6144]{1,0:T(8,128)(2,1)} fusion(bf16[1,6144,512]{2,1,0:T(8,128)(2,1)} %param.12, bf16[448,256]{1,0:T(8,128)(2,1)S(1)} %get-tuple-element.3, bf16[448,256]{1,0:T(8,128)(2,1)S(1)} %get-tuple-element.2), kind=kOutput, calls=%fused_computation.1 | convolution fusion | flops 2822242304 | bytes 12255232 | tf_op jit(solution)/shard_map/dot_general | solution.py:470
  136.1 8.3 %all-to-all-start.2 = ((bf16[8,56,6144]{2,1,0:T(8,128)(2,1)}), bf16[8,56,6144]{2,1,0:T(8,128)(2,1)}, u32[]{:S(2)}, u32[]{:S(2)}) async-start(bf16[8,56,6144]{2,1,0:T(8,128)(2,1)} %bitcast.39), calls=%async_computation.2 | async-start | bytes 11010048 | tf_op jit(solution)/shard_map/all_to_all | solution.py:187
  144.4 6.5 %convolution_convert_fusion = bf16[6144,512]{1,0:T(8,128)(2,1)S(1)} fusion(bf16[448,6144]{1,0:T(8,128)(2,1)} %bitcast.8, bf16[448,256]{1,0:T(8,128)(2,1)S(1)} %get-tuple-element.3, bf16[448,256]{1,0:T(8,128)(2,1)S(1)} %get-tuple-element.2), kind=kOutput, calls=%fused_computation | convolution fusion | flops 2822635520 | bytes 12255232 | tf_op jit(solution)/shard_map/dot_general | solution.py:478
  150.9 53.5 %reduce_rows.1 = f32[192,512]{1,0:T(8,128)S(1)} custom-call(bf16[32,192,512]{2,1,0:T(8,128)(2,1)S(1)} %bitcast.36), custom_call_target="tpu_custom_call" | custom-call | flops 40000000000 | bytes 7000000 | tf_op jit(solution)/shard_map/reduce_rows/pallas_call | solution.py:120
  204.4 4.7 %convolution_convert_fusion.3 = bf16[128,6144]{1,0:T(8,128)(2,1)} fusion(bf16[448,6144]{1,0:T(8,128)(2,1)} %bitcast.12, s32[128]{0:T(128)S(1)} %get-tuple-element.10, s32[128]{0:T(128)S(1)} %get-tuple-element.11), kind=kOutput, calls=%fused_computation.3 | convolution fusion | flops 705601536 | bytes 7078912 | tf_op jit(solution)/shard_map/dot_general | solution.py:474
  209.2 0.7 copy.38
  (13 shorter events, 0.1 us)
Async XLA Ops:
  0.6 13.5 %copy-start.1 = (bf16[128,6144]{1,0:T(8,128)(2,1)S(1)}, bf16[128,6144]{1,0:T(8,128)(2,1)}, u32[]{:S(2)}) copy-start(bf16[128,6144]{1,0:T(8,128)(2,1)} %param.7) | copy-start | bytes 4718596
  2.9 28.4 %all-to-all-start = ((bf16[16,192,256]{2,1,0:T(8,128)(2,1)}), bf16[16,192,256]{2,1,0:T(8,128)(2,1)S(1)}, u32[]{:S(2)}, u32[]{:S(2)}) async-start(bf16[16,192,256]{2,1,0:T(8,128)(2,1)} %broadcast_in_dim.10), calls=%async_computation | async-start | bytes 3145728 | tf_op jit(solution)/shard_map/all_to_all | solution.py:197
  31.4 5.6 %copy-start.2 = (f32[128,2]{0,1:T(2,128)S(1)}, f32[128,2]{0,1:T(2,128)}, u32[]{:S(2)}) copy-start(f32[128,2]{0,1:T(2,128)} %param.11) | copy-start | bytes 3076
  31.4 5.9 %copy-start = (bf16[128,6144]{1,0:T(8,128)(2,1)S(1)}, bf16[128,6144]{1,0:T(8,128)(2,1)}, u32[]{:S(2)}) copy-start(bf16[128,6144]{1,0:T(8,128)(2,1)} %grad_ref.1) | copy-start | bytes 4718596
  31.4 89.2 %all-to-all-start.1 = ((bf16[8,56,6144]{2,1,0:T(8,128)(2,1)}), bf16[8,56,6144]{2,1,0:T(8,128)(2,1)}, u32[]{:S(2)}, u32[]{:S(2)}) async-start(bf16[8,56,6144]{2,1,0:T(8,128)(2,1)} %bitcast.37), calls=%async_computation.1 | async-start | bytes 11010048 | tf_op jit(solution)/shard_map/all_to_all | solution.py:187
  136.1 68.4 %all-to-all-start.2 = ((bf16[8,56,6144]{2,1,0:T(8,128)(2,1)}), bf16[8,56,6144]{2,1,0:T(8,128)(2,1)}, u32[]{:S(2)}, u32[]{:S(2)}) async-start(bf16[8,56,6144]{2,1,0:T(8,128)(2,1)} %bitcast.39), calls=%async_computation.2 | async-start | bytes 11010048 | tf_op jit(solution)/shard_map/all_to_all | solution.py:187

commit v4 on v3

--- a/solution.py
+++ b/solution.py
@@ -198,7 +198,7 @@
     return mine.reshape((planes, experts) + w_down.shape)
 
 
-def relay_kernel(zs, grad_ref, ids_in_ref, gate_ref, weight_ref, slots_ref, out_ref, ids_ref, ids_send, ids_recv,
+def relay_kernel(zs, grad_ref, ids_in_ref, gate_ref, weight_ref, slots_ref, out_ref, ids_ref, turn_ref, ids_send, ids_recv,
                  tail_ref, tail_send, tail_recv, tail_sem, slice_ref, wide_ref, pick_ref, stage_ref, back_ref,
                  own_sem, slice_send, slice_recv, weight_sem, weight_send, weight_recv, back_send, back_recv):
     z, xlo, core = ring_place()
@@ -365,21 +365,22 @@
                 ids_arrival(slot).wait_recv()
                 slice_arrival(slot).wait_recv()
         pick_ref[...] = jnp.zeros_like(pick_ref)
+        for side in range(2):
+            tall = jnp.concatenate([ids_ref[2 * pair + side]] * (tokens // ids_ref.shape[1]), axis=0)
+            turn_ref[pl.ds(side * tokens, tokens), :] = tall.T
 
         def per_expert(e, carry):
-            wide = wide_ref[e]
-            for side in range(2):
-                slot = 2 * pair + side
-                dense = jnp.dot(slice_ref[slot], wide, preferred_element_type=jnp.float32)
-                for k in range(2):
-                    chosen = ids_ref[slot, :, k : k + 1] == e
-                    pick_ref[side, k] = jnp.where(chosen, dense, pick_ref[side, k])
+            both = slice_ref[pl.ds(2 * pair, 2)].reshape(2 * tokens, depth)
+            dense = jnp.dot(both, wide_ref[e], preferred_element_type=jnp.float32)
+            for k in range(2):
+                pick_ref[k] = jnp.where(turn_ref[:, k : k + 1] == e, dense, pick_ref[k])
             return carry
 
         lax.fori_loop(0, experts, per_expert, 0)
         for side in range(2):
             slot = 2 * pair + side
-            stage_ref[slot] = pick_ref[side].astype(stage_ref.dtype)
+            for k in range(2):
+                stage_ref[slot, k] = pick_ref[k, pl.ds(side * tokens, tokens), :].astype(stage_ref.dtype)
             if slot < zs - 1:
                 back_copy(slot).start()
     total = stage_ref[zs - 1].astype(jnp.float32)
@@ -422,6 +423,7 @@
         out_specs=anywhere,
         scratch_shapes=[
             pltpu.VMEM((zs,) + route_ids.shape, route_ids.dtype),
+            pltpu.VMEM((2 * tokens, tokens), route_ids.dtype),
             pairs,
             pairs,
             pltpu.VMEM((experts, tail_rows, hidden), kind),
@@ -430,7 +432,7 @@
             pltpu.SemaphoreType.DMA,
             pltpu.VMEM((zs, tokens, depth), kind),
             pltpu.VMEM((experts, 2 * planes * rows, hidden), kind),
-            pltpu.VMEM((2, 2, tokens, hidden), jnp.float32),
+            pltpu.VMEM((2, 2 * tokens, hidden), jnp.float32),
             pltpu.VMEM((zs, 2, tokens, hidden), kind),
             pltpu.VMEM((zs - 1, 2, tokens, hidden), kind),
             pltpu.SemaphoreType.DMA,
@@ -463,7 +465,8 @@
     zs = lax.axis_size("z")
     weights = plane_weights(w_down[0])
     features = exchange(sent_x, experts, capacity)
-    got_hidden = relay(out_grad, route_ids, gates, weights, slots, zs)
+    id_rows = jnp.pad(route_ids.T, ((0, 6), (0, 0)))
+    got_hidden = relay(out_grad, id_rows, gates, weights, slots, zs)
     back_hidden = got_hidden[:, :capacity].reshape(experts * capacity, hidden).astype(jnp.float32)
     gate_up = jnp.dot(features, weight_in, preferred_element_type=jnp.float32)
     hidden_grad = gated_backward(gate_up, back_hidden)

time: 212 us -> 200 us (0.943)
  Pallas kernels: 137 us -> 125 us
    pallas_call x1, Pallas kernels: 83.3 us -> 72.6 us  [relay(): pl.pallas_call(functools.partial(relay_kernel, zs), out_shape=jax.ShapeDt...]
  transfers between devices with their start and end apart: 3 -> 3, of which waited for: 1 -> 1; matrix products, arithmetic and copies ran while one was open for 7% -> 7% of each run, Pallas kernels for 65% -> 63%
where the time goes in v4:
time: 200 us; the launch traced here: 197 us
  Pallas kernels  125 us (62%)
  matrix products  30.9 us (15%)
  starting transfers between devices  21 us (10%)
  waiting for transfers between devices  13.1 us (7%)
  local copies, waits for them, and re-layouts  6 us (3%)
    pallas_call x1, Pallas kernels, relay(): pl.pallas_call(functools.partial(relay_kernel, zs), out_shape=jax.ShapeDt...  72.6 us
    pallas_call x1, Pallas kernels, reduce_rows(): pl.pallas_call(functools.partial(reduce_kernel, zs, subs), out_shape=jax....  52.1 us
    all_to_all x2, starting transfers between devices, exchange(): lax.all_to_all(rows.reshape(experts, capacity, width), ROW_AXES, split_ax...  13.6 us
    all_to_all x1, waiting for transfers between devices, plane_weights(): lax.all_to_all(copies, ('xlo',) + ROW_AXES, split_axis=0, concat_axis=0,...  13 us
    dot_general x1, matrix products, on_device(): lax.dot_general(hidden_grad, weight_in, (((1,), (1,)), ((), ())), preferr...  8.4 us
    all_to_all x1, starting transfers between devices, plane_weights(): lax.all_to_all(copies, ('xlo',) + ROW_AXES, split_axis=0, concat_axis=0,...  7.45 us
    dot_general x1, matrix products, on_device(): gate_up = jnp.dot(features, weight_in, preferred_element_type=jnp.float32)  6.82 us
    dot_general x1, matrix products, on_device(): lax.dot_general(features, hidden_grad, (((0,), (0,)), ((), ())), preferre...  6.52 us
  transfers between devices with their start and end apart: 3, of which 1 were waited for; matrix products, arithmetic and copies ran while one was open for 7% of the time, Pallas kernels for 63%

profile of v4, /device:TPU:4, one launch (start us, length us, event | category | flops | bytes accessed | tf_op | source)
XLA Modules:
  0.0 197.5 jit_solution(16667219723495475340)
XLA Ops:
  0.6 2.3 %broadcast_in_dim.10 = bf16[16,192,256]{2,1,0:T(8,128)(2,1)} broadcast(bf16[192,256]{1,0:T(8,128)(2,1)} %bitcast.41), dimensions={1,2} | broadcast | bytes 1671168 | tf_op jit(solution)/shard_map/broadcast_in_dim | solution.py:196
  2.9 7.5 %all-to-all-start = ((bf16[16,192,256]{2,1,0:T(8,128)(2,1)}), bf16[16,192,256]{2,1,0:T(8,128)(2,1)S(1)}, u32[]{:S(2)}, u32[]{:S(2)}) async-start(bf16[16,192,256]{2,1,0:T(8,128)(2,1)} %broadcast_in_dim.10), calls=%async_computation | async-start | bytes 3145728 | tf_op jit(solution)/shard_map/all_to_all | solution.py:197
  10.4 0.8 copy.29
  11.2 0.8 copy.25
  12.0 0.1 eq.76
  12.1 0.2 fusion.5
  12.3 0.1 convert_element_type.44
  12.5 0.1 copy.26
  12.5 0.7 multiply_add_fusion
  13.3 0.9 mul.47
  14.1 4.2 %convolution_convert_fusion.2 = bf16[448,6144]{1,0:T(8,128)(2,1)} fusion(f32[16,8,48,128]{3,2,1,0:T(8,128)S(1)} %bitcast.39, bf16[128,6144]{1,0:T(8,128)(2,1)S(1)} %copy-done.1, s32[128]{0:T(128)S(1)} %get-tuple-element.10, s32[128]{0:T(128)S(1)} %get-tuple-element.11), kind=kOutput, calls=%fused_computation.2 | convolution fusion | flops 709926912 | bytes 10224640 | tf_op jit(solution)/shard_map/dot_general | solution.py:463
  18.3 13.0 %all-to-all-done = bf16[16,192,256]{2,1,0:T(8,128)(2,1)S(1)} async-done(((bf16[16,192,256]{2,1,0:T(8,128)(2,1)}), bf16[16,192,256]{2,1,0:T(8,128)(2,1)S(1)}, u32[]{:S(2)}, u32[]{:S(2)}) %all-to-all-start) | async-done | bytes 1572896 | tf_op jit(solution)/shard_map/all_to_all | solution.py:197
  31.4 5.6 %all-to-all-start.1 = ((bf16[8,56,6144]{2,1,0:T(8,128)(2,1)}), bf16[8,56,6144]{2,1,0:T(8,128)(2,1)}, u32[]{:S(2)}, u32[]{:S(2)}) async-start(bf16[8,56,6144]{2,1,0:T(8,128)(2,1)} %bitcast.38), calls=%async_computation.1 | async-start | bytes 11010048 | tf_op jit(solution)/shard_map/all_to_all | solution.py:187
  37.0 0.1 copy.28.gate_ref
  37.3 0.1 add_convert_fusion.slots_ref
  37.3 72.6 %relay.1 = bf16[8,64,256]{2,1,0:T(8,128)(2,1)S(1)} custom-call(bf16[128,6144]{1,0:T(8,128)(2,1)S(1)} %copy-done, s32[8,128]{1,0:T(8,128)S(1)} %pad.4.ids_in_ref, f32[128,2]{1,0:T(8,128)S(1)} %copy.28.gate_ref, bf16[2,8,192,256]{3,2,1,0:T(8,128)(2,1)S(1)} %bitcast.35, bf16[512,256]{1,0:T(8,128)(2,1)S(1)} %add_convert_fusion.slots_ref), custom_call_target="tpu_custom_call" | custom-call | flops 40000000000 | bytes 7000000 | tf_op jit(solution)/shard_map/relay/pallas_call | solution.py:419
  109.9 6.8 %fusion.1 = f32[448,512]{1,0:T(8,128)S(1)} fusion(bf16[448,6144]{1,0:T(8,128)(2,1)} %bitcast.9, bf16[1,6144,512]{2,1,0:T(8,128)(2,1)} %param.12), kind=kOutput, calls=%fused_computation.5 | convolution fusion | flops 2818572288 | bytes 12713984 | tf_op jit(solution)/shard_map/dot_general | solution.py:471
  116.8 0.2 fusion.8
  117.0 8.4 %convolution_convert_fusion.1 = bf16[448,6144]{1,0:T(8,128)(2,1)} fusion(bf16[1,6144,512]{2,1,0:T(8,128)(2,1)} %param.12, bf16[448,256]{1,0:T(8,128)(2,1)S(1)} %get-tuple-element.3, bf16[448,256]{1,0:T(8,128)(2,1)S(1)} %get-tuple-element.2), kind=kOutput, calls=%fused_computation.1 | convolution fusion | flops 2822242304 | bytes 12255232 | tf_op jit(solution)/shard_map/dot_general | solution.py:473
  125.4 7.9 %all-to-all-start.2 = ((bf16[8,56,6144]{2,1,0:T(8,128)(2,1)}), bf16[8,56,6144]{2,1,0:T(8,128)(2,1)}, u32[]{:S(2)}, u32[]{:S(2)}) async-start(bf16[8,56,6144]{2,1,0:T(8,128)(2,1)} %bitcast.40), calls=%async_computation.2 | async-start | bytes 11010048 | tf_op jit(solution)/shard_map/all_to_all | solution.py:187
  133.4 6.5 %convolution_convert_fusion = bf16[6144,512]{1,0:T(8,128)(2,1)S(1)} fusion(bf16[448,6144]{1,0:T(8,128)(2,1)} %bitcast.9, bf16[448,256]{1,0:T(8,128)(2,1)S(1)} %get-tuple-element.3, bf16[448,256]{1,0:T(8,128)(2,1)S(1)} %get-tuple-element.2), kind=kOutput, calls=%fused_computation | convolution fusion | flops 2822635520 | bytes 12255232 | tf_op jit(solution)/shard_map/dot_general | solution.py:481
  139.9 52.1 %reduce_rows.1 = f32[192,512]{1,0:T(8,128)S(1)} custom-call(bf16[32,192,512]{2,1,0:T(8,128)(2,1)S(1)} %bitcast.37), custom_call_target="tpu_custom_call" | custom-call | flops 40000000000 | bytes 7000000 | tf_op jit(solution)/shard_map/reduce_rows/pallas_call | solution.py:120
  192.0 4.7 %convolution_convert_fusion.3 = bf16[128,6144]{1,0:T(8,128)(2,1)} fusion(bf16[448,6144]{1,0:T(8,128)(2,1)} %bitcast.13, s32[128]{0:T(128)S(1)} %get-tuple-element.10, s32[128]{0:T(128)S(1)} %get-tuple-element.11), kind=kOutput, calls=%fused_computation.3 | convolution fusion | flops 705601536 | bytes 7078912 | tf_op jit(solution)/shard_map/dot_general | solution.py:477
  196.7 0.7 copy.34
  (16 shorter events, 0.2 us)
Async XLA Ops:
  0.6 13.5 %copy-start.1 = (bf16[128,6144]{1,0:T(8,128)(2,1)S(1)}, bf16[128,6144]{1,0:T(8,128)(2,1)}, u32[]{:S(2)}) copy-start(bf16[128,6144]{1,0:T(8,128)(2,1)} %param.7) | copy-start | bytes 4718596
  2.9 28.4 %all-to-all-start = ((bf16[16,192,256]{2,1,0:T(8,128)(2,1)}), bf16[16,192,256]{2,1,0:T(8,128)(2,1)S(1)}, u32[]{:S(2)}, u32[]{:S(2)}) async-start(bf16[16,192,256]{2,1,0:T(8,128)(2,1)} %broadcast_in_dim.10), calls=%async_computation | async-start | bytes 3145728 | tf_op jit(solution)/shard_map/all_to_all | solution.py:197
  31.4 5.6 %copy-start.3 = (f32[128,2]{0,1:T(2,128)S(1)}, f32[128,2]{0,1:T(2,128)}, u32[]{:S(2)}) copy-start(f32[128,2]{0,1:T(2,128)} %param.11) | copy-start | bytes 3076
  31.4 5.7 %copy-start.2 = (s32[128,2]{0,1:T(2,128)S(1)}, s32[128,2]{0,1:T(2,128)}, u32[]{:S(2)}) copy-start(s32[128,2]{0,1:T(2,128)} %param.10) | copy-start | bytes 3076
  31.4 5.9 %copy-start = (bf16[128,6144]{1,0:T(8,128)(2,1)S(1)}, bf16[128,6144]{1,0:T(8,128)(2,1)}, u32[]{:S(2)}) copy-start(bf16[128,6144]{1,0:T(8,128)(2,1)} %grad_ref.1) | copy-start | bytes 4718596
  31.4 78.5 %all-to-all-start.1 = ((bf16[8,56,6144]{2,1,0:T(8,128)(2,1)}), bf16[8,56,6144]{2,1,0:T(8,128)(2,1)}, u32[]{:S(2)}, u32[]{:S(2)}) async-start(bf16[8,56,6144]{2,1,0:T(8,128)(2,1)} %bitcast.38), calls=%async_computation.1 | async-start | bytes 11010048 | tf_op jit(solution)/shard_map/all_to_all | solution.py:187
  125.4 66.5 %all-to-all-start.2 = ((bf16[8,56,6144]{2,1,0:T(8,128)(2,1)}), bf16[8,56,6144]{2,1,0:T(8,128)(2,1)}, u32[]{:S(2)}, u32[]{:S(2)}) async-start(bf16[8,56,6144]{2,1,0:T(8,128)(2,1)} %bitcast.40), calls=%async_computation.2 | async-start | bytes 11010048 | tf_op jit(solution)/shard_map/all_to_all | solution.py:187

commit v5 on v4

--- a/solution.py
+++ b/solution.py
@@ -142,36 +142,6 @@
     )(part.reshape(dp_count, rows, width))
 
 
-def dispatch_masks(route_ids, experts, capacity, stride):
-    tokens = route_ids.shape[0]
-    flat_ids = route_ids.reshape(-1)
-    slot_total = flat_ids.shape[0]
-    onehot = flat_ids[:, None] == jnp.arange(experts, dtype=jnp.int32)[None, :]
-    order = jnp.arange(slot_total, dtype=jnp.int32)
-    before = (order[:, None] > order[None, :]).astype(jnp.bfloat16)
-    earlier = jnp.dot(before, onehot.astype(jnp.bfloat16), preferred_element_type=jnp.float32)
-    ranking = jnp.sum(jnp.where(onehot, earlier, 0.0), axis=1).astype(jnp.int32)
-
-    def match(pitch):
-        target = (flat_ids * pitch + ranking).reshape(tokens, 2)
-        rows = jnp.arange(experts * pitch, dtype=jnp.int32)[:, None]
-        return rows == target[:, 0][None, :], rows == target[:, 1][None, :]
-
-    first, second = match(capacity)
-    slots = jnp.concatenate(match(stride), axis=1).astype(jnp.bfloat16)
-    return (first | second).astype(jnp.bfloat16), slots
-
-
-def dequantize(stash_rows, scale_rows):
-    row_total = stash_rows.shape[0]
-    blocks = scale_rows.shape[1]
-    scaled = (
-        stash_rows.reshape(row_total, blocks, -1).astype(jnp.float32)
-        * scale_rows.astype(jnp.float32)[:, :, None]
-    )
-    return scaled.reshape(row_total, -1).astype(jnp.bfloat16)
-
-
 def gated_backward(gate_up, back_hidden):
     hidden = back_hidden.shape[1]
     gate_value = gate_up[:, :hidden]
@@ -190,12 +160,145 @@
     return moved.reshape(experts * capacity, width)
 
 
-def plane_weights(w_down):
-    planes = lax.axis_size("xlo")
+def front_kernel(xs, ys, capacity, stride, pieces, ids_ref, stash_ref, scale_ref, weight_ref,
+                 rows_ref, plane_ref, picks_ref, slots_ref,
+                 build_ref, build_sem, keep_sem, y_send, y_recv, x_send, x_recv, yx_send, yx_recv, xy_send, xy_recv):
+    xlo, xhi, y = lax.axis_index("xlo"), lax.axis_index("xhi"), lax.axis_index("y")
+    x = xhi * 2 + xlo
+    tokens, width = stash_ref.shape
+    half = weight_ref.shape[0] // 2
+    step = width // pieces
+
+    def x_at(shift):
+        return lax.rem(x + shift + xs, xs)
+
+    def y_at(shift):
+        return lax.rem(y + shift + ys, ys)
+
+    def x_place(shift):
+        return {"xlo": lax.rem(x_at(shift), 2), "xhi": x_at(shift) // 2}
+
+    def y_place(shift):
+        return {"y": y_at(shift)}
+
+    def landed(xx, yy, part):
+        return plane_ref.at[lax.rem(xx, 2), (xx // 2) * ys + yy, pl.ds(part * half, half), :]
+
+    def moved(source, target, send, recv, device):
+        return pltpu.make_async_remote_copy(
+            src_ref=source, dst_ref=target, send_sem=send, recv_sem=recv, device_id=device, device_id_type=MESH
+        )
+
+    greet([x_place(k) for k in range(1, xs)] + [y_place(k) for k in range(1, ys)])
+    own = [weight_ref.at[pl.ds(part * half, half), :] for part in range(2)]
+    keep = pltpu.make_async_copy(weight_ref, plane_ref.at[xlo, xhi * ys + y], keep_sem)
+    keep.start()
+    sends, waits = [], []
+
+    def send(copy):
+        copy.start()
+        sends.append(copy)
+
+    for k in range(1, ys):
+        send(moved(own[0], landed(x, y, 0), y_send.at[k - 1], y_recv.at[k - 1], y_place(k)))
+    for k in range(1, xs):
+        send(moved(own[1], landed(x, y, 1), x_send.at[k - 1], x_recv.at[k - 1], x_place(k)))
+    for k in range(1, xs):
+        send(moved(own[0], landed(x, y, 0), yx_send.at[0, k - 1], yx_recv.at[0, k - 1], x_place(k)))
+    for k in range(1, ys):
+        send(moved(own[1], landed(x, y, 1), xy_send.at[0, k - 1], xy_recv.at[0, k - 1], y_place(k)))
+
+    expert = lax.broadcasted_iota(jnp.int32, ids_ref.shape, 0)
+    first, second = ids_ref[0:1, :], ids_ref[1:2, :]
+    named = jnp.where((expert == first) | (expert == second), 1.0, 0.0).astype(jnp.bfloat16)
+    ahead = jnp.where(
+        lax.broadcasted_iota(jnp.int32, (tokens, tokens), 0) < lax.broadcasted_iota(jnp.int32, (tokens, tokens), 1),
+        1.0, 0.0,
+    ).astype(jnp.bfloat16)
+    earlier = jnp.dot(named, ahead, preferred_element_type=jnp.float32)
+    row = lax.broadcasted_iota(jnp.int32, (slots_ref.shape[0], tokens), 0).astype(jnp.float32)
+    short = row[: rows_ref.shape[0]]
+    hit = None
+    for k, chosen in enumerate((first, second)):
+        rank = jnp.sum(jnp.where(expert == chosen, earlier, 0.0), axis=0, keepdims=True)
+        wide = row == chosen.astype(jnp.float32) * stride + rank
+        slots_ref[:, k * tokens : (k + 1) * tokens] = jnp.where(wide, 1.0, 0.0).astype(slots_ref.dtype)
+        match = short == chosen.astype(jnp.float32) * capacity + rank
+        hit = match if hit is None else hit | match
+    picks_ref[...] = jnp.where(hit, 1.0, 0.0).astype(picks_ref.dtype)
+    block = lax.broadcasted_iota(jnp.int32, (scale_ref.shape[1], step), 0)
+    lane = lax.broadcasted_iota(jnp.int32, (scale_ref.shape[1], step), 1) // (width // scale_ref.shape[1])
+    per_step = step * scale_ref.shape[1] // width
+
+    def build(piece, carry):
+        spread = jnp.where(block == lane + piece * per_step, 1.0, 0.0).astype(jnp.bfloat16)
+        scale = jnp.dot(scale_ref[...], spread, preferred_element_type=jnp.float32)
+        span = pl.ds(pl.multiple_of(piece * step, step), step)
+        value = (stash_ref[:, span].astype(jnp.float32) * scale).astype(jnp.bfloat16)
+        placed = jnp.dot(picks_ref[...], value, preferred_element_type=jnp.float32)
+        build_ref[:, span] = placed.astype(build_ref.dtype)
+        return carry
+
+    lax.fori_loop(0, pieces // 2, build, 0)
+    for j in range(1, ys):
+        piece = landed(x, y_at(-j), 0)
+        moved(own[0], piece, y_send.at[j - 1], y_recv.at[j - 1], y_place(j)).wait_recv()
+        for k in range(1, xs):
+            send(moved(piece, piece, yx_send.at[j, k - 1], yx_recv.at[j, k - 1], x_place(k)))
+    for j in range(1, xs):
+        piece = landed(x_at(-j), y, 1)
+        moved(own[1], piece, x_send.at[j - 1], x_recv.at[j - 1], x_place(j)).wait_recv()
+        for k in range(1, ys):
+            send(moved(piece, piece, xy_send.at[j, k - 1], xy_recv.at[j, k - 1], y_place(k)))
+    lax.fori_loop(pieces // 2, pieces, build, 0)
+    put = pltpu.make_async_copy(build_ref, rows_ref, build_sem)
+    put.start()
+    for j in range(ys):
+        for k in range(1, xs):
+            piece = landed(x_at(-k), y_at(-j), 0)
+            moved(own[0], piece, yx_send.at[j, k - 1], yx_recv.at[j, k - 1], x_place(k)).wait_recv()
+    for j in range(xs):
+        for k in range(1, ys):
+            piece = landed(x_at(-j), y_at(-k), 1)
+            moved(own[1], piece, xy_send.at[j, k - 1], xy_recv.at[j, k - 1], y_place(k)).wait_recv()
+    for copy in sends:
+        copy.wait_send()
+    keep.wait()
+    put.wait()
+
+
+def front(id_rows, stash, scales, w_down, capacity, stride):
+    tokens, width = stash.shape
+    rows, hidden = w_down.shape
     experts = lax.axis_size(ROW_AXES)
-    copies = jnp.broadcast_to(w_down[None], (planes * experts,) + w_down.shape)
-    mine = lax.all_to_all(copies, ("xlo",) + ROW_AXES, split_axis=0, concat_axis=0, tiled=True)
-    return mine.reshape((planes, experts) + w_down.shape)
+    xs, ys = 2 * lax.axis_size("xhi"), lax.axis_size("y")
+    kind = stash.dtype
+    vmem = pl.BlockSpec(memory_space=pltpu.VMEM)
+    anywhere = pl.BlockSpec(memory_space=pl.ANY)
+    semaphores = []
+    for shape in ((ys - 1,), (xs - 1,), (ys, xs - 1), (xs, ys - 1)):
+        semaphores += [pltpu.SemaphoreType.DMA(shape), pltpu.SemaphoreType.DMA(shape)]
+    return pl.pallas_call(
+        functools.partial(front_kernel, xs, ys, capacity, stride, 8),
+        out_shape=(
+            jax.ShapeDtypeStruct((experts * capacity, width), kind),
+            jax.ShapeDtypeStruct((2, experts, rows, hidden), kind),
+            jax.ShapeDtypeStruct((experts * capacity, tokens), kind),
+            jax.ShapeDtypeStruct((experts * stride, 2 * tokens), kind),
+        ),
+        in_specs=[vmem, vmem, vmem, vmem],
+        out_specs=(anywhere, anywhere, vmem, vmem),
+        scratch_shapes=[
+            pltpu.VMEM((experts * capacity, width), kind),
+            pltpu.SemaphoreType.DMA,
+            pltpu.SemaphoreType.DMA,
+        ] + semaphores,
+        compiler_params=pltpu.CompilerParams(
+            collective_id=3, has_side_effects=True, vmem_limit_bytes=60 * 1024 * 1024
+        ),
+        cost_estimate=pl.CostEstimate(flops=20_000_000_000, bytes_accessed=10_000_000, transcendentals=0),
+        name="front",
+    )(id_rows, stash, scales, w_down)
 
 
 def relay_kernel(zs, grad_ref, ids_in_ref, gate_ref, weight_ref, slots_ref, out_ref, ids_ref, turn_ref, ids_send, ids_recv,
@@ -459,13 +562,11 @@
     dp_count = lax.axis_size(COLUMN_AXES)
     capacity = min(tokens, 7 * tokens // (2 * experts))
     stride = -(-capacity // 16) * 16
-    picks, slots = dispatch_masks(route_ids, experts, capacity, stride)
-    sent_x = jnp.dot(picks, dequantize(stash, scales), preferred_element_type=jnp.float32).astype(jnp.bfloat16)
+    id_rows = jnp.pad(route_ids.T, ((0, 6), (0, 0)))
+    sent_x, weights, picks, slots = front(id_rows, stash, scales, w_down[0], capacity, stride)
     weight_in = w_gate_up[0]
     zs = lax.axis_size("z")
-    weights = plane_weights(w_down[0])
     features = exchange(sent_x, experts, capacity)
-    id_rows = jnp.pad(route_ids.T, ((0, 6), (0, 0)))
     got_hidden = relay(out_grad, id_rows, gates, weights, slots, zs)
     back_hidden = got_hidden[:, :capacity].reshape(experts * capacity, hidden).astype(jnp.float32)
     gate_up = jnp.dot(features, weight_in, preferred_element_type=jnp.float32)

time: 200 us -> 191 us (0.955)
  Pallas kernels: 125 us -> 144 us
  waiting for transfers between devices: 13.1 us -> 0.01 us
  starting transfers between devices: 21 us -> 14.9 us
  matrix products: 30.9 us -> 26.4 us
  local copies, waits for them, and re-layouts: 6 us -> 3.6 us
    pallas_call x0 -> x1, Pallas kernels: none -> 18.5 us  [front(): pl.pallas_call(functools.partial(front_kernel, xs, ys, capacity, stride,...]
    all_to_all x1 -> x0, waiting for transfers between devices: 13 us -> none  [plane_weights(): lax.all_to_all(copies, ('xlo',) + ROW_AXES, split_axis=0, concat_axis=0,...]
    all_to_all x1 -> x0, starting transfers between devices: 7.45 us -> none  [plane_weights(): lax.all_to_all(copies, ('xlo',) + ROW_AXES, split_axis=0, concat_axis=0,...]
    dot_general x2 -> x0, matrix products: 4.41 us -> none  [the longest x1 4.21 us: on_device(): jnp.dot(picks, dequantize(stash, scales), preferred_element_type=jnp.floa...]
    broadcast_in_dim x1 -> x0, local copies, waits for them, and re-layouts: 2.3 us -> none  [plane_weights(): copies = jnp.broadcast_to(w_down[None], (planes * experts,) + w_down.shape)]
  transfers between devices with their start and end apart: 3 -> 2, of which waited for: 1 -> 0; matrix products, arithmetic and copies ran while one was open for 7% -> 3% of each run, Pallas kernels for 63% -> 66%
where the time goes in v5:
time: 191 us; the launch traced here: 190 us
  Pallas kernels  144 us (75%)
  matrix products  26.4 us (14%)
  starting transfers between devices  14.9 us (8%)
  local copies, waits for them, and re-layouts  3.6 us (2%)
    pallas_call x1, Pallas kernels, relay(): pl.pallas_call(functools.partial(relay_kernel, zs), out_shape=jax.ShapeDt...  72.2 us
    pallas_call x1, Pallas kernels, reduce_rows(): pl.pallas_call(functools.partial(reduce_kernel, zs, subs), out_shape=jax....  53 us
    pallas_call x1, Pallas kernels, front(): pl.pallas_call(functools.partial(front_kernel, xs, ys, capacity, stride,...  18.5 us
    all_to_all x2, starting transfers between devices, exchange(): lax.all_to_all(rows.reshape(experts, capacity, width), ROW_AXES, split_ax...  14.9 us
    dot_general x1, matrix products, on_device(): lax.dot_general(hidden_grad, weight_in, (((1,), (1,)), ((), ())), preferr...  8.38 us
    dot_general x1, matrix products, on_device(): gate_up = jnp.dot(features, weight_in, preferred_element_type=jnp.float32)  6.82 us
    dot_general x1, matrix products, on_device(): lax.dot_general(features, hidden_grad, (((0,), (0,)), ((), ())), preferre...  6.51 us
    dot_general x1, matrix products, on_device(): lax.dot_general(picks, returned, (((0,), (0,)), ((), ())), preferred_elem...  4.73 us
  transfers between devices with their start and end apart: 2, of which 0 were waited for; matrix products, arithmetic and copies ran while one was open for 3% of the time, Pallas kernels for 66%

profile of v5, /device:TPU:4, one launch (start us, length us, event | category | flops | bytes accessed | tf_op | source)
XLA Modules:
  0.0 189.7 jit_solution(10868584353784938019)
XLA Ops:
  0.6 1.4 copy.9.scale_ref
  2.1 1.3 pad.4.ids_ref.ids_in_ref
  3.3 18.5 %front.1 = (bf16[448,6144]{1,0:T(8,128)(2,1)}, bf16[2,8,192,256]{3,2,1,0:T(8,128)(2,1)}, bf16[448,128]{1,0:T(8,128)(2,1)}, bf16[512,256]{1,0:T(8,128)(2,1)}) custom-call(s32[8,128]{1,0:T(8,128)} %pad.4.ids_ref.ids_in_ref, bf16[128,6144]{1,0:T(8,128)(2,1)} %stash_ref.1, bf16[128,48]{1,0:T(8,128)(2,1)} %copy.9.scale_ref, bf16[192,256]{1,0:T(8,128)(2,1)} %bitcast.26), custom_call_target="tpu_custom_call" | custom-call | flops 20000000000 | bytes 10000000 | tf_op jit(solution)/shard_map/front/pallas_call | solution.py:281
  21.8 0.0 copy-start.5
  21.8 0.0 copy-start
  21.9 0.0 copy-start.1
  21.9 0.0 copy-start.2
  21.9 0.0 copy-start.3
  21.9 7.0 %all-to-all-start = ((bf16[8,56,6144]{2,1,0:T(8,128)(2,1)}), bf16[8,56,6144]{2,1,0:T(8,128)(2,1)}, u32[]{:S(2)}, u32[]{:S(2)}) async-start(bf16[8,56,6144]{2,1,0:T(8,128)(2,1)} %bitcast.23), calls=%async_computation | async-start | bytes 11010048 | tf_op jit(solution)/shard_map/all_to_all | solution.py:157
  28.8 0.0 copy-done.5
  28.8 0.1 copy.10.gate_ref
  29.0 0.0 copy-done
  29.0 72.2 %relay.1 = bf16[8,64,256]{2,1,0:T(8,128)(2,1)S(1)} custom-call(bf16[128,6144]{1,0:T(8,128)(2,1)S(1)} %copy-done.1, s32[8,128]{1,0:T(8,128)S(1)} %copy-done, f32[128,2]{1,0:T(8,128)S(1)} %copy.10.gate_ref, bf16[2,8,192,256]{3,2,1,0:T(8,128)(2,1)S(1)} %copy-done.2, bf16[512,256]{1,0:T(8,128)(2,1)S(1)} %copy-done.3), custom_call_target="tpu_custom_call" | custom-call | flops 40000000000 | bytes 7000000 | tf_op jit(solution)/shard_map/relay/pallas_call | solution.py:522
  101.2 0.0 all-to-all-done
  101.2 6.8 %fusion.1 = f32[448,512]{1,0:T(8,128)S(1)} fusion(bf16[448,6144]{1,0:T(8,128)(2,1)} %bitcast.4, bf16[1,6144,512]{2,1,0:T(8,128)(2,1)} %param.12), kind=kOutput, calls=%fused_computation.4 | convolution fusion | flops 2818572288 | bytes 12713984 | tf_op jit(solution)/shard_map/dot_general | solution.py:572
  108.1 0.2 fusion.5
  108.3 8.4 %convolution_convert_fusion.1 = bf16[448,6144]{1,0:T(8,128)(2,1)} fusion(bf16[1,6144,512]{2,1,0:T(8,128)(2,1)} %param.12, bf16[448,256]{1,0:T(8,128)(2,1)S(1)} %get-tuple-element.11, bf16[448,256]{1,0:T(8,128)(2,1)S(1)} %get-tuple-element.10), kind=kOutput, calls=%fused_computation.1 | convolution fusion | flops 2822242304 | bytes 12255232 | tf_op jit(solution)/shard_map/dot_general | solution.py:574
  116.7 7.9 %all-to-all-start.1 = ((bf16[8,56,6144]{2,1,0:T(8,128)(2,1)}), bf16[8,56,6144]{2,1,0:T(8,128)(2,1)}, u32[]{:S(2)}, u32[]{:S(2)}) async-start(bf16[8,56,6144]{2,1,0:T(8,128)(2,1)} %bitcast.24), calls=%async_computation.1 | async-start | bytes 11010048 | tf_op jit(solution)/shard_map/all_to_all | solution.py:157
  124.6 6.5 %convolution_convert_fusion = bf16[6144,512]{1,0:T(8,128)(2,1)S(1)} fusion(bf16[448,6144]{1,0:T(8,128)(2,1)} %bitcast.4, bf16[448,256]{1,0:T(8,128)(2,1)S(1)} %get-tuple-element.11, bf16[448,256]{1,0:T(8,128)(2,1)S(1)} %get-tuple-element.10), kind=kOutput, calls=%fused_computation | convolution fusion | flops 2822635520 | bytes 12255232 | tf_op jit(solution)/shard_map/dot_general | solution.py:582
  131.2 0.0 copy-start.4
  131.2 53.0 %reduce_rows.1 = f32[192,512]{1,0:T(8,128)S(1)} custom-call(bf16[32,192,512]{2,1,0:T(8,128)(2,1)S(1)} %bitcast.22), custom_call_target="tpu_custom_call" | custom-call | flops 40000000000 | bytes 7000000 | tf_op jit(solution)/shard_map/reduce_rows/pallas_call | solution.py:120
  184.2 0.0 all-to-all-done.1
  184.2 4.7 %convolution_convert_fusion.2 = bf16[128,6144]{1,0:T(8,128)(2,1)} fusion(bf16[448,128]{1,0:T(8,128)(2,1)S(1)} %copy-done.4, bf16[448,6144]{1,0:T(8,128)(2,1)} %bitcast.8), kind=kOutput, calls=%fused_computation.2 | convolution fusion | flops 705429504 | bytes 7192576 | tf_op jit(solution)/shard_map/dot_general | solution.py:578
  188.9 0.7 copy.12
  (5 shorter events, 0.0 us)
Async XLA Ops:
  21.8 7.0 %copy-start.5 = (f32[128,2]{0,1:T(2,128)S(1)}, f32[128,2]{0,1:T(2,128)}, u32[]{:S(2)}) copy-start(f32[128,2]{0,1:T(2,128)} %param.11) | copy-start | bytes 3076
  21.8 7.1 %copy-start = (s32[8,128]{1,0:T(8,128)S(1)}, s32[8,128]{1,0:T(8,128)}, u32[]{:S(2)}) copy-start(s32[8,128]{1,0:T(8,128)} %pad.4.ids_ref.ids_in_ref) | copy-start | bytes 12292
  21.9 7.1 %copy-start.1 = (bf16[128,6144]{1,0:T(8,128)(2,1)S(1)}, bf16[128,6144]{1,0:T(8,128)(2,1)}, u32[]{:S(2)}) copy-start(bf16[128,6144]{1,0:T(8,128)(2,1)} %grad_ref.1) | copy-start | bytes 4718596
  21.9 7.1 %copy-start.2 = (bf16[2,8,192,256]{3,2,1,0:T(8,128)(2,1)S(1)}, bf16[2,8,192,256]{3,2,1,0:T(8,128)(2,1)}, u32[]{:S(2)}) copy-start(bf16[2,8,192,256]{3,2,1,0:T(8,128)(2,1)} %get-tuple-element.7.weight_ref) | copy-start | bytes 4718596
  21.9 7.1 %copy-start.3 = (bf16[512,256]{1,0:T(8,128)(2,1)S(1)}, bf16[512,256]{1,0:T(8,128)(2,1)}, u32[]{:S(2)}) copy-start(bf16[512,256]{1,0:T(8,128)(2,1)} %get-tuple-element.8.slots_ref) | copy-start | bytes 786436
  21.9 79.3 %all-to-all-start = ((bf16[8,56,6144]{2,1,0:T(8,128)(2,1)}), bf16[8,56,6144]{2,1,0:T(8,128)(2,1)}, u32[]{:S(2)}, u32[]{:S(2)}) async-start(bf16[8,56,6144]{2,1,0:T(8,128)(2,1)} %bitcast.23), calls=%async_computation | async-start | bytes 11010048 | tf_op jit(solution)/shard_map/all_to_all | solution.py:157
  116.7 67.5 %all-to-all-start.1 = ((bf16[8,56,6144]{2,1,0:T(8,128)(2,1)}), bf16[8,56,6144]{2,1,0:T(8,128)(2,1)}, u32[]{:S(2)}, u32[]{:S(2)}) async-start(bf16[8,56,6144]{2,1,0:T(8,128)(2,1)} %bitcast.24), calls=%async_computation.1 | async-start | bytes 11010048 | tf_op jit(solution)/shard_map/all_to_all | solution.py:157
  131.2 53.0 %copy-start.4 = (bf16[448,128]{1,0:T(8,128)(2,1)S(1)}, bf16[448,128]{1,0:T(8,128)(2,1)}, u32[]{:S(2)}) copy-start(bf16[448,128]{1,0:T(8,128)(2,1)} %get-tuple-element.6) | copy-start | bytes 344068

commit v6 on v5

--- a/solution.py
+++ b/solution.py
@@ -160,12 +160,27 @@
     return moved.reshape(experts * capacity, width)
 
 
-def front_kernel(xs, ys, capacity, stride, pieces, ids_ref, stash_ref, scale_ref, weight_ref,
-                 rows_ref, plane_ref, picks_ref, slots_ref,
+def ring_offsets(zs):
+    offsets = []
+    for d in range(1, zs // 2):
+        offsets += [-d, d]
+    return offsets + [zs // 2, 0]
+
+
+def near_slots(zs):
+    return min(4, zs - 2)
+
+
+def front_kernel(zs, xs, ys, capacity, stride, pieces, ids_ref, stash_ref, scale_ref, weight_ref, grad_ref,
+                 rows_ref, plane_ref, picks_ref, slots_ref, tile_ref, near_ref, near_send, near_recv,
                  build_ref, build_sem, keep_sem, y_send, y_recv, x_send, x_recv, yx_send, yx_recv, xy_send, xy_recv):
     xlo, xhi, y = lax.axis_index("xlo"), lax.axis_index("xhi"), lax.axis_index("y")
     x = xhi * 2 + xlo
+    z = lax.axis_index("z")
     tokens, width = stash_ref.shape
+    depth = width // zs
+    near = near_slots(zs)
+    offsets = ring_offsets(zs)
     half = weight_ref.shape[0] // 2
     step = width // pieces
 
@@ -189,7 +204,14 @@
             src_ref=source, dst_ref=target, send_sem=send, recv_sem=recv, device_id=device, device_id_type=MESH
         )
 
-    greet([x_place(k) for k in range(1, xs)] + [y_place(k) for k in range(1, ys)])
+    def z_at(slot):
+        return lax.rem(z + offsets[slot] + zs, zs)
+
+    greet(
+        [x_place(k) for k in range(1, xs)]
+        + [y_place(k) for k in range(1, ys)]
+        + [{"z": z_at(slot)} for slot in range(near)]
+    )
     own = [weight_ref.at[pl.ds(part * half, half), :] for part in range(2)]
     keep = pltpu.make_async_copy(weight_ref, plane_ref.at[xlo, xhi * ys + y], keep_sem)
     keep.start()
@@ -208,8 +230,13 @@
     for k in range(1, ys):
         send(moved(own[1], landed(x, y, 1), xy_send.at[0, k - 1], xy_recv.at[0, k - 1], y_place(k)))
 
-    expert = lax.broadcasted_iota(jnp.int32, ids_ref.shape, 0)
+    for slot in range(near):
+        columns = grad_ref.at[:, pl.ds(pl.multiple_of(z_at(slot) * depth, depth), depth)]
+        send(moved(columns, near_ref.at[slot ^ 1], near_send.at[slot], near_recv.at[slot ^ 1], {"z": z_at(slot)}))
+
+    expert = lax.broadcasted_iota(jnp.int32, tile_ref.shape, 0)
     first, second = ids_ref[0:1, :], ids_ref[1:2, :]
+    tile_ref[...] = jnp.where(expert == 0, first, second)
     named = jnp.where((expert == first) | (expert == second), 1.0, 0.0).astype(jnp.bfloat16)
     ahead = jnp.where(
         lax.broadcasted_iota(jnp.int32, (tokens, tokens), 0) < lax.broadcasted_iota(jnp.int32, (tokens, tokens), 1),
@@ -226,13 +253,16 @@
         match = short == chosen.astype(jnp.float32) * capacity + rank
         hit = match if hit is None else hit | match
     picks_ref[...] = jnp.where(hit, 1.0, 0.0).astype(picks_ref.dtype)
-    block = lax.broadcasted_iota(jnp.int32, (scale_ref.shape[1], step), 0)
-    lane = lax.broadcasted_iota(jnp.int32, (scale_ref.shape[1], step), 1) // (width // scale_ref.shape[1])
-    per_step = step * scale_ref.shape[1] // width
+    blocks = scale_ref.shape[0]
+    block = lax.broadcasted_iota(jnp.int32, (blocks, step), 0)
+    lane = lax.broadcasted_iota(jnp.int32, (blocks, step), 1) // (width // blocks)
+    per_step = step * blocks // width
 
     def build(piece, carry):
         spread = jnp.where(block == lane + piece * per_step, 1.0, 0.0).astype(jnp.bfloat16)
-        scale = jnp.dot(scale_ref[...], spread, preferred_element_type=jnp.float32)
+        scale = lax.dot_general(
+            scale_ref[...], spread, (((0,), (0,)), ((), ())), preferred_element_type=jnp.float32
+        )
         span = pl.ds(pl.multiple_of(piece * step, step), step)
         value = (stash_ref[:, span].astype(jnp.float32) * scale).astype(jnp.bfloat16)
         placed = jnp.dot(picks_ref[...], value, preferred_element_type=jnp.float32)
@@ -261,17 +291,21 @@
         for k in range(1, ys):
             piece = landed(x_at(-j), y_at(-k), 1)
             moved(own[1], piece, xy_send.at[j, k - 1], xy_recv.at[j, k - 1], y_place(k)).wait_recv()
+    for slot in range(near):
+        landing = near_ref.at[slot]
+        moved(landing, landing, near_send.at[slot], near_recv.at[slot], {"z": z_at(slot)}).wait_recv()
     for copy in sends:
         copy.wait_send()
     keep.wait()
     put.wait()
 
 
-def front(id_rows, stash, scales, w_down, capacity, stride):
+def front(id_rows, stash, scale_rows, w_down, out_grad, capacity, stride):
     tokens, width = stash.shape
     rows, hidden = w_down.shape
     experts = lax.axis_size(ROW_AXES)
-    xs, ys = 2 * lax.axis_size("xhi"), lax.axis_size("y")
+    zs, xs, ys = lax.axis_size("z"), 2 * lax.axis_size("xhi"), lax.axis_size("y")
+    near = near_slots(zs)
     kind = stash.dtype
     vmem = pl.BlockSpec(memory_space=pltpu.VMEM)
     anywhere = pl.BlockSpec(memory_space=pl.ANY)
@@ -279,16 +313,20 @@
     for shape in ((ys - 1,), (xs - 1,), (ys, xs - 1), (xs, ys - 1)):
         semaphores += [pltpu.SemaphoreType.DMA(shape), pltpu.SemaphoreType.DMA(shape)]
     return pl.pallas_call(
-        functools.partial(front_kernel, xs, ys, capacity, stride, 8),
+        functools.partial(front_kernel, zs, xs, ys, capacity, stride, 8),
         out_shape=(
             jax.ShapeDtypeStruct((experts * capacity, width), kind),
             jax.ShapeDtypeStruct((2, experts, rows, hidden), kind),
             jax.ShapeDtypeStruct((experts * capacity, tokens), kind),
             jax.ShapeDtypeStruct((experts * stride, 2 * tokens), kind),
+            jax.ShapeDtypeStruct((8, tokens), id_rows.dtype),
+            jax.ShapeDtypeStruct((near, tokens, width // zs), kind),
         ),
-        in_specs=[vmem, vmem, vmem, vmem],
-        out_specs=(anywhere, anywhere, vmem, vmem),
+        in_specs=[vmem, vmem, vmem, vmem, anywhere],
+        out_specs=(anywhere, anywhere, vmem, vmem, vmem, anywhere),
         scratch_shapes=[
+            pltpu.SemaphoreType.DMA((near,)),
+            pltpu.SemaphoreType.DMA((near,)),
             pltpu.VMEM((experts * capacity, width), kind),
             pltpu.SemaphoreType.DMA,
             pltpu.SemaphoreType.DMA,
@@ -298,12 +336,12 @@
         ),
         cost_estimate=pl.CostEstimate(flops=20_000_000_000, bytes_accessed=10_000_000, transcendentals=0),
         name="front",
-    )(id_rows, stash, scales, w_down)
-
-
-def relay_kernel(zs, grad_ref, ids_in_ref, gate_ref, weight_ref, slots_ref, out_ref, ids_ref, turn_ref, ids_send, ids_recv,
+    )(id_rows, stash, scale_rows, w_down, out_grad)
+
+
+def relay_kernel(zs, grad_ref, near_ref, ids_in_ref, gate_ref, weight_ref, slots_ref, out_ref, ids_ref, turn_ref, ids_send, ids_recv,
                  tail_ref, tail_send, tail_recv, tail_sem, slice_ref, wide_ref, pick_ref, stage_ref, back_ref,
-                 own_sem, slice_send, slice_recv, weight_sem, weight_send, weight_recv, back_send, back_recv):
+                 own_sem, near_sem, slice_send, slice_recv, weight_sem, weight_send, weight_recv, back_send, back_recv):
     z, xlo, core = ring_place()
     tokens = slice_ref.shape[1]
     depth = slice_ref.shape[2]
@@ -320,10 +358,8 @@
     experts = weight_ref.shape[1]
     rows = weight_ref.shape[2]
     half = zs // 2
-    offsets = []
-    for d in range(1, half):
-        offsets += [-d, d]
-    offsets += [half, 0]
+    offsets = ring_offsets(zs)
+    near = near_slots(zs)
     twin = place(z, xlo, 1 - core)
 
     def peer(offset):
@@ -446,11 +482,12 @@
         )
 
     keeps = [pltpu.make_async_copy(grad_ref.at[:, columns(0)], slice_ref.at[zs - 1], own_sem)]
+    keeps.append(pltpu.make_async_copy(near_ref, slice_ref.at[pl.ds(0, near)], near_sem))
     for plane in range(2):
         keeps.append(pltpu.make_async_copy(weight_ref.at[plane], weight_rows(plane, core), weight_sem.at[plane]))
     for slot in range(zs - 1):
         ids_copy(slot).start()
-    for slot in range(zs - 1):
+    for slot in range(near, zs - 1):
         slice_copy(slot).start()
     for plane in range(2):
         weight_copy(plane).start()
@@ -466,7 +503,8 @@
             slot = 2 * pair + side
             if slot < zs - 1:
                 ids_arrival(slot).wait_recv()
-                slice_arrival(slot).wait_recv()
+                if slot >= near:
+                    slice_arrival(slot).wait_recv()
         pick_ref[...] = jnp.zeros_like(pick_ref)
         for side in range(2):
             tall = jnp.concatenate([ids_ref[2 * pair + side]] * (tokens // ids_ref.shape[1]), axis=0)
@@ -499,7 +537,8 @@
     keep_tail.start()
     for slot in range(zs - 1):
         ids_copy(slot).wait_send()
-        slice_copy(slot).wait_send()
+        if slot >= near:
+            slice_copy(slot).wait_send()
         back_copy(slot).wait_send()
     for plane in range(2):
         weight_copy(plane).wait_send()
@@ -509,7 +548,7 @@
     keep_tail.wait()
 
 
-def relay(out_grad, route_ids, gates, weights, slots, zs):
+def relay(out_grad, near, route_ids, gates, weights, slots, zs):
     tokens, feature_width = out_grad.shape
     planes, experts, rows, hidden = weights.shape
     depth = feature_width // zs
@@ -522,7 +561,7 @@
     return pl.pallas_call(
         functools.partial(relay_kernel, zs),
         out_shape=jax.ShapeDtypeStruct((experts, tail_rows, hidden), kind),
-        in_specs=[anywhere, vmem, vmem, anywhere, vmem],
+        in_specs=[anywhere, anywhere, vmem, vmem, anywhere, vmem],
         out_specs=anywhere,
         scratch_shapes=[
             pltpu.VMEM((zs,) + route_ids.shape, route_ids.dtype),
@@ -539,6 +578,7 @@
             pltpu.VMEM((zs, 2, tokens, hidden), kind),
             pltpu.VMEM((zs - 1, 2, tokens, hidden), kind),
             pltpu.SemaphoreType.DMA,
+            pltpu.SemaphoreType.DMA,
             pairs,
             pairs,
             pltpu.SemaphoreType.DMA((2,)),
@@ -552,7 +592,7 @@
         ),
         cost_estimate=pl.CostEstimate(flops=40_000_000_000, bytes_accessed=7_000_000, transcendentals=0),
         name="relay",
-    )(out_grad, route_ids, gates, weights, slots)
+    )(out_grad, near, route_ids, gates, weights, slots)
 
 
 def on_device(stash, scales, out_grad, route_ids, gates, w_gate_up, w_down):
@@ -562,12 +602,13 @@
     dp_count = lax.axis_size(COLUMN_AXES)
     capacity = min(tokens, 7 * tokens // (2 * experts))
     stride = -(-capacity // 16) * 16
-    id_rows = jnp.pad(route_ids.T, ((0, 6), (0, 0)))
-    sent_x, weights, picks, slots = front(id_rows, stash, scales, w_down[0], capacity, stride)
+    sent_x, weights, picks, slots, id_rows, near = front(
+        route_ids.T, stash, scales.T, w_down[0], out_grad, capacity, stride
+    )
     weight_in = w_gate_up[0]
     zs = lax.axis_size("z")
     features = exchange(sent_x, experts, capacity)
-    got_hidden = relay(out_grad, id_rows, gates, weights, slots, zs)
+    got_hidden = relay(out_grad, near, id_rows, gates, weights, slots, zs)
     back_hidden = got_hidden[:, :capacity].reshape(experts * capacity, hidden).astype(jnp.float32)
     gate_up = jnp.dot(features, weight_in, preferred_element_type=jnp.float32)
     hidden_grad = gated_backward(gate_up, back_hidden)

time: 191 us -> 190 us (level)
  Pallas kernels: 144 us -> 146 us
    pallas_call x1, Pallas kernels: 72.2 us -> 63.1 us  [relay(): pl.pallas_call(functools.partial(relay_kernel, zs), out_shape=jax.ShapeDt...]
    pallas_call x1, Pallas kernels: 18.5 us -> 24.7 us  [front(): pl.pallas_call(functools.partial(front_kernel, zs, xs, ys, capacity, stri...]
    pallas_call x1, Pallas kernels: 53 us -> 58.1 us  [reduce_rows(): pl.pallas_call(functools.partial(reduce_kernel, zs, subs), out_shape=jax....]
  transfers between devices with their start and end apart: 2 -> 2, of which waited for: 0 -> 0; matrix products, arithmetic and copies ran while one was open for 3% -> 3% of each run, Pallas kernels for 66% -> 64%
where the time goes in v6:
time: 190 us
  Pallas kernels  146 us (77%)
  matrix products  26.5 us (14%)
  starting transfers between devices  14.4 us (8%)
  local copies, waits for them, and re-layouts  2.03 us (1%)
    pallas_call x1, Pallas kernels, relay(): pl.pallas_call(functools.partial(relay_kernel, zs), out_shape=jax.ShapeDt...  63.1 us
    pallas_call x1, Pallas kernels, reduce_rows(): pl.pallas_call(functools.partial(reduce_kernel, zs, subs), out_shape=jax....  58.1 us
    pallas_call x1, Pallas kernels, front(): pl.pallas_call(functools.partial(front_kernel, zs, xs, ys, capacity, stri...  24.7 us
    all_to_all x2, starting transfers between devices, exchange(): lax.all_to_all(rows.reshape(experts, capacity, width), ROW_AXES, split_ax...  14.4 us
    dot_general x1, matrix products, on_device(): lax.dot_general(hidden_grad, weight_in, (((1,), (1,)), ((), ())), preferr...  8.41 us
    dot_general x1, matrix products, on_device(): gate_up = jnp.dot(features, weight_in, preferred_element_type=jnp.float32)  6.82 us
    dot_general x1, matrix products, on_device(): lax.dot_general(features, hidden_grad, (((0,), (0,)), ((), ())), preferre...  6.5 us
    dot_general x1, matrix products, on_device(): lax.dot_general(picks, returned, (((0,), (0,)), ((), ())), preferred_elem...  4.72 us
  transfers between devices with their start and end apart: 2, of which 0 were waited for; matrix products, arithmetic and copies ran while one was open for 3% of the time, Pallas kernels for 64%

profile of v6, /device:TPU:4, one launch (start us, length us, event | category | flops | bytes accessed | tf_op | source)
XLA Modules:
  0.0 189.9 jit_solution(6039506357764885801)
XLA Ops:
  0.6 24.7 %front.1 = (bf16[448,6144]{1,0:T(8,128)(2,1)}, bf16[2,8,192,256]{3,2,1,0:T(8,128)(2,1)}, bf16[448,128]{1,0:T(8,128)(2,1)}, bf16[512,256]{1,0:T(8,128)(2,1)}, s32...) custom-call(s32[2,128]{1,0:T(2,128)} %bitcast.28, bf16[128,6144]{1,0:T(8,128)(2,1)} %stash_ref.1, bf16[48,128]{1,0:T(8,128)(2,1)} %bitcast.27, ...), custom_call_target="tpu_custom_call" | custom-call | flops 20000000000 | bytes 10000000 | tf_op jit(solution)/shard_map/front/pallas_call | solution.py:315
  25.3 0.0 copy-start.6
  25.3 0.0 copy-start
  25.3 0.0 copy-start.1
  25.4 0.0 copy-start.3
  25.4 0.0 copy-start.4
  25.4 7.3 %all-to-all-start = ((bf16[8,56,6144]{2,1,0:T(8,128)(2,1)}), bf16[8,56,6144]{2,1,0:T(8,128)(2,1)}, u32[]{:S(2)}, u32[]{:S(2)}) async-start(bf16[8,56,6144]{2,1,0:T(8,128)(2,1)} %bitcast.24), calls=%async_computation | async-start | bytes 11010048 | tf_op jit(solution)/shard_map/all_to_all | solution.py:157
  32.6 0.0 copy-done.6
  32.6 0.1 copy.9.gate_ref
  32.7 0.0 copy-done
  32.7 0.0 copy-done.1
  32.8 0.0 copy-done.3
  32.8 1.1 copy-done.2
  33.9 63.1 %relay.1 = bf16[8,64,256]{2,1,0:T(8,128)(2,1)S(1)} custom-call(bf16[128,6144]{1,0:T(8,128)(2,1)S(1)} %copy-done, bf16[4,128,768]{2,1,0:T(8,128)(2,1)S(1)} %copy-done.2, s32[8,128]{1,0:T(8,128)S(1)} %copy-done.4, f32[128,2]{1,0:T(8,128)S(1)} %copy.9.gate_ref, bf16[2,8,192,256]{3,2,1,0:T(8,128)(2,1)S(1)} %copy-done.1, bf16[512,256]{1,0:T(8,128)(2,1)S(1)} %copy-done.3), custom_call_target="tpu_custom_call" | custom-call | flops 40000000000 | bytes 7000000 | tf_op jit(solution)/shard_map/relay/pallas_call | solution.py:561
  97.1 0.0 all-to-all-done
  97.1 6.8 %fusion.1 = f32[448,512]{1,0:T(8,128)S(1)} fusion(bf16[448,6144]{1,0:T(8,128)(2,1)} %bitcast.5, bf16[1,6144,512]{2,1,0:T(8,128)(2,1)} %param.12), kind=kOutput, calls=%fused_computation.4 | convolution fusion | flops 2818572288 | bytes 12713984 | tf_op jit(solution)/shard_map/dot_general | solution.py:613
  103.9 0.2 fusion.5
  104.2 8.4 %convolution_convert_fusion.1 = bf16[448,6144]{1,0:T(8,128)(2,1)} fusion(bf16[1,6144,512]{2,1,0:T(8,128)(2,1)} %param.12, bf16[448,256]{1,0:T(8,128)(2,1)S(1)} %get-tuple-element.15, bf16[448,256]{1,0:T(8,128)(2,1)S(1)} %get-tuple-element.14), kind=kOutput, calls=%fused_computation.1 | convolution fusion | flops 2822242304 | bytes 12255232 | tf_op jit(solution)/shard_map/dot_general | solution.py:615
  112.6 7.2 %all-to-all-start.1 = ((bf16[8,56,6144]{2,1,0:T(8,128)(2,1)}), bf16[8,56,6144]{2,1,0:T(8,128)(2,1)}, u32[]{:S(2)}, u32[]{:S(2)}) async-start(bf16[8,56,6144]{2,1,0:T(8,128)(2,1)} %bitcast.25), calls=%async_computation.1 | async-start | bytes 11010048 | tf_op jit(solution)/shard_map/all_to_all | solution.py:157
  119.8 6.5 %convolution_convert_fusion = bf16[6144,512]{1,0:T(8,128)(2,1)S(1)} fusion(bf16[448,6144]{1,0:T(8,128)(2,1)} %bitcast.5, bf16[448,256]{1,0:T(8,128)(2,1)S(1)} %get-tuple-element.15, bf16[448,256]{1,0:T(8,128)(2,1)S(1)} %get-tuple-element.14), kind=kOutput, calls=%fused_computation | convolution fusion | flops 2822635520 | bytes 12255232 | tf_op jit(solution)/shard_map/dot_general | solution.py:623
  126.3 58.1 %reduce_rows.1 = f32[192,512]{1,0:T(8,128)S(1)} custom-call(bf16[32,192,512]{2,1,0:T(8,128)(2,1)S(1)} %bitcast.23), custom_call_target="tpu_custom_call" | custom-call | flops 40000000000 | bytes 7000000 | tf_op jit(solution)/shard_map/reduce_rows/pallas_call | solution.py:120
  184.4 0.0 all-to-all-done.1
  184.4 4.7 %convolution_convert_fusion.2 = bf16[128,6144]{1,0:T(8,128)(2,1)} fusion(bf16[448,128]{1,0:T(8,128)(2,1)S(1)} %copy-done.5, bf16[448,6144]{1,0:T(8,128)(2,1)} %bitcast.9), kind=kOutput, calls=%fused_computation.2 | convolution fusion | flops 705429504 | bytes 7192576 | tf_op jit(solution)/shard_map/dot_general | solution.py:619
  189.1 0.7 copy.11
  (5 shorter events, 0.0 us)
Async XLA Ops:
  25.3 7.3 %copy-start.6 = (f32[128,2]{0,1:T(2,128)S(1)}, f32[128,2]{0,1:T(2,128)}, u32[]{:S(2)}) copy-start(f32[128,2]{0,1:T(2,128)} %param.11) | copy-start | bytes 3076
  25.3 7.4 %copy-start = (bf16[128,6144]{1,0:T(8,128)(2,1)S(1)}, bf16[128,6144]{1,0:T(8,128)(2,1)}, u32[]{:S(2)}) copy-start(bf16[128,6144]{1,0:T(8,128)(2,1)} %grad_ref.3) | copy-start | bytes 4718596
  25.3 7.4 %copy-start.1 = (bf16[2,8,192,256]{3,2,1,0:T(8,128)(2,1)S(1)}, bf16[2,8,192,256]{3,2,1,0:T(8,128)(2,1)}, u32[]{:S(2)}) copy-start(bf16[2,8,192,256]{3,2,1,0:T(8,128)(2,1)} %get-tuple-element.11.weight_ref) | copy-start | bytes 4718596
  25.4 7.4 %copy-start.3 = (bf16[512,256]{1,0:T(8,128)(2,1)S(1)}, bf16[512,256]{1,0:T(8,128)(2,1)}, u32[]{:S(2)}) copy-start(bf16[512,256]{1,0:T(8,128)(2,1)} %get-tuple-element.12.slots_ref) | copy-start | bytes 786436
  25.4 7.4 %copy-start.4 = (s32[8,128]{1,0:T(8,128)S(1)}, s32[8,128]{1,0:T(8,128)}, u32[]{:S(2)}) copy-start(s32[8,128]{1,0:T(8,128)} %get-tuple-element.10.ids_in_ref) | copy-start | bytes 12292
  25.4 71.7 %all-to-all-start = ((bf16[8,56,6144]{2,1,0:T(8,128)(2,1)}), bf16[8,56,6144]{2,1,0:T(8,128)(2,1)}, u32[]{:S(2)}, u32[]{:S(2)}) async-start(bf16[8,56,6144]{2,1,0:T(8,128)(2,1)} %bitcast.24), calls=%async_computation | async-start | bytes 11010048 | tf_op jit(solution)/shard_map/all_to_all | solution.py:157
  32.8 1.1 copy-start.2
  112.6 71.8 %all-to-all-start.1 = ((bf16[8,56,6144]{2,1,0:T(8,128)(2,1)}), bf16[8,56,6144]{2,1,0:T(8,128)(2,1)}, u32[]{:S(2)}, u32[]{:S(2)}) async-start(bf16[8,56,6144]{2,1,0:T(8,128)(2,1)} %bitcast.25), calls=%async_computation.1 | async-start | bytes 11010048 | tf_op jit(solution)/shard_map/all_to_all | solution.py:157
  126.3 58.1 %copy-start.5 = (bf16[448,128]{1,0:T(8,128)(2,1)S(1)}, bf16[448,128]{1,0:T(8,128)(2,1)}, u32[]{:S(2)}) copy-start(bf16[448,128]{1,0:T(8,128)(2,1)} %get-tuple-element.8) | copy-start | bytes 344068

commit v7 on v6

--- a/solution.py
+++ b/solution.py
@@ -168,7 +168,7 @@
 
 
 def near_slots(zs):
-    return min(4, zs - 2)
+    return min(2, zs - 2)
 
 
 def front_kernel(zs, xs, ys, capacity, stride, pieces, ids_ref, stash_ref, scale_ref, weight_ref, grad_ref,
@@ -269,7 +269,7 @@
         build_ref[:, span] = placed.astype(build_ref.dtype)
         return carry
 
-    lax.fori_loop(0, pieces // 2, build, 0)
+    lax.fori_loop(0, pieces // 4, build, 0)
     for j in range(1, ys):
         piece = landed(x, y_at(-j), 0)
         moved(own[0], piece, y_send.at[j - 1], y_recv.at[j - 1], y_place(j)).wait_recv()
@@ -280,7 +280,7 @@
         moved(own[1], piece, x_send.at[j - 1], x_recv.at[j - 1], x_place(j)).wait_recv()
         for k in range(1, ys):
             send(moved(piece, piece, xy_send.at[j, k - 1], xy_recv.at[j, k - 1], y_place(k)))
-    lax.fori_loop(pieces // 2, pieces, build, 0)
+    lax.fori_loop(pieces // 4, pieces, build, 0)
     put = pltpu.make_async_copy(build_ref, rows_ref, build_sem)
     put.start()
     for j in range(ys):

time: 190 us -> 188 us (0.989)
  Pallas kernels: 146 us -> 143 us
    pallas_call x1, Pallas kernels: 58.1 us -> 55.7 us  [reduce_rows(): pl.pallas_call(functools.partial(reduce_kernel, zs, subs), out_shape=jax....]
  transfers between devices with their start and end apart: 2 -> 2, of which waited for: 0 -> 0; matrix products, arithmetic and copies ran while one was open for 3% -> 4% of each run, Pallas kernels for 64% -> 64%
where the time goes in v7:
time: 188 us; the launch traced here: 186 us
  Pallas kernels  143 us (76%)
  matrix products  26.4 us (14%)
  starting transfers between devices  14 us (7%)
  local copies, waits for them, and re-layouts  1.89 us (1%)
    pallas_call x1, Pallas kernels, relay(): pl.pallas_call(functools.partial(relay_kernel, zs), out_shape=jax.ShapeDt...  64.2 us
    pallas_call x1, Pallas kernels, reduce_rows(): pl.pallas_call(functools.partial(reduce_kernel, zs, subs), out_shape=jax....  55.7 us
    pallas_call x1, Pallas kernels, front(): pl.pallas_call(functools.partial(front_kernel, zs, xs, ys, capacity, stri...  23.1 us
    all_to_all x2, starting transfers between devices, exchange(): lax.all_to_all(rows.reshape(experts, capacity, width), ROW_AXES, split_ax...  14 us
    dot_general x1, matrix products, on_device(): lax.dot_general(hidden_grad, weight_in, (((1,), (1,)), ((), ())), preferr...  8.38 us
    dot_general x1, matrix products, on_device(): gate_up = jnp.dot(features, weight_in, preferred_element_type=jnp.float32)  6.82 us
    dot_general x1, matrix products, on_device(): lax.dot_general(features, hidden_grad, (((0,), (0,)), ((), ())), preferre...  6.51 us
    dot_general x1, matrix products, on_device(): lax.dot_general(picks, returned, (((0,), (0,)), ((), ())), preferred_elem...  4.72 us
  transfers between devices with their start and end apart: 2, of which 0 were waited for; matrix products, arithmetic and copies ran while one was open for 4% of the time, Pallas kernels for 64%

profile of v7, /device:TPU:4, one launch (start us, length us, event | category | flops | bytes accessed | tf_op | source)
XLA Modules:
  0.0 186.3 jit_solution(18341918043416975805)
XLA Ops:
  0.6 23.1 %front.1 = (bf16[448,6144]{1,0:T(8,128)(2,1)}, bf16[2,8,192,256]{3,2,1,0:T(8,128)(2,1)}, bf16[448,128]{1,0:T(8,128)(2,1)}, bf16[512,256]{1,0:T(8,128)(2,1)}, s32...) custom-call(s32[2,128]{1,0:T(2,128)} %bitcast.28, bf16[128,6144]{1,0:T(8,128)(2,1)} %stash_ref.1, bf16[48,128]{1,0:T(8,128)(2,1)} %bitcast.27, ...), custom_call_target="tpu_custom_call" | custom-call | flops 20000000000 | bytes 10000000 | tf_op jit(solution)/shard_map/front/pallas_call | solution.py:315
  23.7 0.0 copy-start.6
  23.7 0.0 copy-start
  23.8 0.0 copy-start.1
  23.8 0.0 copy-start.3
  23.8 0.0 copy-start.4
  23.8 6.0 %all-to-all-start = ((bf16[8,56,6144]{2,1,0:T(8,128)(2,1)}), bf16[8,56,6144]{2,1,0:T(8,128)(2,1)}, u32[]{:S(2)}, u32[]{:S(2)}) async-start(bf16[8,56,6144]{2,1,0:T(8,128)(2,1)} %bitcast.24), calls=%async_computation | async-start | bytes 11010048 | tf_op jit(solution)/shard_map/all_to_all | solution.py:157
  29.8 0.0 copy-done.6
  29.8 0.1 copy.9.gate_ref
  29.9 0.0 copy-done
  29.9 0.0 copy-done.1
  29.9 1.0 copy-done.2
  30.9 64.2 %relay.1 = bf16[8,64,256]{2,1,0:T(8,128)(2,1)S(1)} custom-call(bf16[128,6144]{1,0:T(8,128)(2,1)S(1)} %copy-done, bf16[2,128,768]{2,1,0:T(8,128)(2,1)S(1)} %copy-done.2, s32[8,128]{1,0:T(8,128)S(1)} %copy-done.4, f32[128,2]{1,0:T(8,128)S(1)} %copy.9.gate_ref, bf16[2,8,192,256]{3,2,1,0:T(8,128)(2,1)S(1)} %copy-done.1, bf16[512,256]{1,0:T(8,128)(2,1)S(1)} %copy-done.3), custom_call_target="tpu_custom_call" | custom-call | flops 40000000000 | bytes 7000000 | tf_op jit(solution)/shard_map/relay/pallas_call | solution.py:561
  95.1 0.0 all-to-all-done
  95.1 6.8 %fusion.1 = f32[448,512]{1,0:T(8,128)S(1)} fusion(bf16[448,6144]{1,0:T(8,128)(2,1)} %bitcast.5, bf16[1,6144,512]{2,1,0:T(8,128)(2,1)} %param.12), kind=kOutput, calls=%fused_computation.4 | convolution fusion | flops 2818572288 | bytes 12713984 | tf_op jit(solution)/shard_map/dot_general | solution.py:613
  102.0 0.2 fusion.5
  102.2 8.4 %convolution_convert_fusion.1 = bf16[448,6144]{1,0:T(8,128)(2,1)} fusion(bf16[1,6144,512]{2,1,0:T(8,128)(2,1)} %param.12, bf16[448,256]{1,0:T(8,128)(2,1)S(1)} %get-tuple-element.15, bf16[448,256]{1,0:T(8,128)(2,1)S(1)} %get-tuple-element.14), kind=kOutput, calls=%fused_computation.1 | convolution fusion | flops 2822242304 | bytes 12255232 | tf_op jit(solution)/shard_map/dot_general | solution.py:615
  110.6 8.0 %all-to-all-start.1 = ((bf16[8,56,6144]{2,1,0:T(8,128)(2,1)}), bf16[8,56,6144]{2,1,0:T(8,128)(2,1)}, u32[]{:S(2)}, u32[]{:S(2)}) async-start(bf16[8,56,6144]{2,1,0:T(8,128)(2,1)} %bitcast.25), calls=%async_computation.1 | async-start | bytes 11010048 | tf_op jit(solution)/shard_map/all_to_all | solution.py:157
  118.6 6.5 %convolution_convert_fusion = bf16[6144,512]{1,0:T(8,128)(2,1)S(1)} fusion(bf16[448,6144]{1,0:T(8,128)(2,1)} %bitcast.5, bf16[448,256]{1,0:T(8,128)(2,1)S(1)} %get-tuple-element.15, bf16[448,256]{1,0:T(8,128)(2,1)S(1)} %get-tuple-element.14), kind=kOutput, calls=%fused_computation | convolution fusion | flops 2822635520 | bytes 12255232 | tf_op jit(solution)/shard_map/dot_general | solution.py:623
  125.1 0.0 copy-start.5
  125.1 55.7 %reduce_rows.1 = f32[192,512]{1,0:T(8,128)S(1)} custom-call(bf16[32,192,512]{2,1,0:T(8,128)(2,1)S(1)} %bitcast.23), custom_call_target="tpu_custom_call" | custom-call | flops 40000000000 | bytes 7000000 | tf_op jit(solution)/shard_map/reduce_rows/pallas_call | solution.py:120
  180.8 0.0 all-to-all-done.1
  180.8 4.7 %convolution_convert_fusion.2 = bf16[128,6144]{1,0:T(8,128)(2,1)} fusion(bf16[448,128]{1,0:T(8,128)(2,1)S(1)} %copy-done.5, bf16[448,6144]{1,0:T(8,128)(2,1)} %bitcast.9), kind=kOutput, calls=%fused_computation.2 | convolution fusion | flops 705429504 | bytes 7192576 | tf_op jit(solution)/shard_map/dot_general | solution.py:619
  185.5 0.7 copy.11
  (5 shorter events, 0.0 us)
Async XLA Ops:
  23.7 6.0 %copy-start.6 = (f32[128,2]{0,1:T(2,128)S(1)}, f32[128,2]{0,1:T(2,128)}, u32[]{:S(2)}) copy-start(f32[128,2]{0,1:T(2,128)} %param.11) | copy-start | bytes 3076
  23.7 6.1 %copy-start = (bf16[128,6144]{1,0:T(8,128)(2,1)S(1)}, bf16[128,6144]{1,0:T(8,128)(2,1)}, u32[]{:S(2)}) copy-start(bf16[128,6144]{1,0:T(8,128)(2,1)} %grad_ref.3) | copy-start | bytes 4718596
  23.8 6.1 %copy-start.1 = (bf16[2,8,192,256]{3,2,1,0:T(8,128)(2,1)S(1)}, bf16[2,8,192,256]{3,2,1,0:T(8,128)(2,1)}, u32[]{:S(2)}) copy-start(bf16[2,8,192,256]{3,2,1,0:T(8,128)(2,1)} %get-tuple-element.11.weight_ref) | copy-start | bytes 4718596
  23.8 6.1 %copy-start.3 = (bf16[512,256]{1,0:T(8,128)(2,1)S(1)}, bf16[512,256]{1,0:T(8,128)(2,1)}, u32[]{:S(2)}) copy-start(bf16[512,256]{1,0:T(8,128)(2,1)} %get-tuple-element.12.slots_ref) | copy-start | bytes 786436
  23.8 6.1 %copy-start.4 = (s32[8,128]{1,0:T(8,128)S(1)}, s32[8,128]{1,0:T(8,128)}, u32[]{:S(2)}) copy-start(s32[8,128]{1,0:T(8,128)} %get-tuple-element.10.ids_in_ref) | copy-start | bytes 12292
  23.8 71.3 %all-to-all-start = ((bf16[8,56,6144]{2,1,0:T(8,128)(2,1)}), bf16[8,56,6144]{2,1,0:T(8,128)(2,1)}, u32[]{:S(2)}, u32[]{:S(2)}) async-start(bf16[8,56,6144]{2,1,0:T(8,128)(2,1)} %bitcast.24), calls=%async_computation | async-start | bytes 11010048 | tf_op jit(solution)/shard_map/all_to_all | solution.py:157
  29.9 1.0 copy-start.2
  110.6 70.2 %all-to-all-start.1 = ((bf16[8,56,6144]{2,1,0:T(8,128)(2,1)}), bf16[8,56,6144]{2,1,0:T(8,128)(2,1)}, u32[]{:S(2)}, u32[]{:S(2)}) async-start(bf16[8,56,6144]{2,1,0:T(8,128)(2,1)} %bitcast.25), calls=%async_computation.1 | async-start | bytes 11010048 | tf_op jit(solution)/shard_map/all_to_all | solution.py:157
  125.1 55.7 %copy-start.5 = (bf16[448,128]{1,0:T(8,128)(2,1)S(1)}, bf16[448,128]{1,0:T(8,128)(2,1)}, u32[]{:S(2)}) copy-start(bf16[448,128]{1,0:T(8,128)(2,1)} %get-tuple-element.8) | copy-start | bytes 344068
